TPU v7x, 128 devices: a whole 4x4x4 slice. The times are simulated.
128 devices in a mesh: row: 8 (over x, z_lo), col: 16 (over y, z_hi, core).
Axes of the slice: x: 4, y: 4, z: 4 (z_hi: 2, z_lo: 2; z = z_hi * 2 + z_lo), core: 2. Of those that a mesh axis runs over, the one named last changes fastest.
Arguments:
- cam_jac: bfloat16 [2, 2, 6, 2048, 1024], P(None, None, None, ('row', 'col')), may hold values from -0.09375 to 0.09375
- pt_jac: bfloat16 [2, 2, 3, 2048, 1024], P(None, None, None, ('row', 'col')), may hold values from -6 to 6
- resid: bfloat16 [2, 2, 2048, 1024], P(None, None, ('row', 'col')), may hold values from -6 to 6
- partner: int32 [2048, 1024], P(('row', 'col')), may hold values from 0 to 2047, as said below
- count: int32 [2048], P(('row', 'col')), may hold values from 512 to 1024
- tile_map: int32 [2048], replicated, may hold values from 0 to 2047, as said below
Outputs:
- coupling: bfloat16 [6, 6, 2048, 2048], P(None, None, 'row', 'col')
- camera_update: float32 [6, 2048], P(None, 'row')
- residual: float32 [6, 2048], P(None, 'row')
Inputs may be any that keep to these rules, and one draw needn't show every extreme that they name: partner[a, t] is never a. `tile_map`: a permutation of the tile positions; of the 16 consecutive scenes of each device, exactly 2 have positions in each block of 256 consecutive positions.
All inputs are finite; a program needn't handle non-finite values.
Results may differ from a plain program's by a relative error of at most 0.0015.
Values may be sent and summed in bfloat16 or wider, within the bound.
A program may use at most 64 MiB of HBM per device.

v0:
```python
import jax
import jax.numpy as jnp
from jax import lax
from jax.sharding import PartitionSpec as P

ITERS = 3


CAMERA_DAMPING = 1.0
POINT_DAMPING = 1.0


def cross_product(first_vec, second_vec):
    return jnp.stack(
        [
            first_vec[1] * second_vec[2] - first_vec[2] * second_vec[1],
            first_vec[2] * second_vec[0] - first_vec[0] * second_vec[2],
            first_vec[0] * second_vec[1] - first_vec[1] * second_vec[0],
        ],
        axis=0,
    )


def point_terms(camera, points_jac, errors):
    camera = camera.astype(jnp.float32)
    points_jac = points_jac.astype(jnp.float32)
    errors = errors.astype(jnp.float32)
    own_jac, other_jac = (camera[0], camera[1])
    own_point, other_point = (points_jac[0], points_jac[1])
    own_error, other_error = (errors[0], errors[1])
    point_hessian = jnp.sum(own_point[:, :, None] * own_point[:, None, :], axis=0)
    point_hessian = point_hessian + jnp.sum(
        other_point[:, :, None] * other_point[:, None, :], axis=0
    )
    point_hessian = point_hessian + POINT_DAMPING * jnp.eye(3, dtype=jnp.float32)[:, :, None, None]
    first_row, second_row, third_row = (point_hessian[0], point_hessian[1], point_hessian[2])
    cofactor_first = cross_product(second_row, third_row)
    cofactor_second = cross_product(third_row, first_row)
    cofactor_third = cross_product(first_row, second_row)
    determinant = jnp.sum(first_row * cofactor_first, axis=0)
    inverse = jnp.stack([cofactor_first, cofactor_second, cofactor_third], axis=1) / determinant
    w_own = jnp.sum(own_jac[:, :, None] * own_point[:, None, :], axis=0)
    w_other = jnp.sum(other_jac[:, :, None] * other_point[:, None, :], axis=0)
    point_rhs = -(
        jnp.sum(own_point * own_error[:, None], axis=0)
        + jnp.sum(other_point * other_error[:, None], axis=0)
    )
    own_vi = jnp.sum(w_own[:, :, None] * inverse[None, :, :], axis=1)
    other_vi = jnp.sum(w_other[:, :, None] * inverse[None, :, :], axis=1)
    diag_own = jnp.sum(own_jac[:, :, None] * own_jac[:, None, :], axis=0) - jnp.sum(
        own_vi[:, None, :] * w_own[None, :, :], axis=2
    )
    diag_other = jnp.sum(other_jac[:, :, None] * other_jac[:, None, :], axis=0) - jnp.sum(
        other_vi[:, None, :] * w_other[None, :, :], axis=2
    )
    link = -jnp.sum(own_vi[:, None, :] * w_other[None, :, :], axis=2)
    grad_own = -jnp.sum(own_jac * own_error[:, None], axis=0) - jnp.sum(
        own_vi * point_rhs[None], axis=1
    )
    grad_other = -jnp.sum(other_jac * other_error[:, None], axis=0) - jnp.sum(
        other_vi * point_rhs[None], axis=1
    )
    return (diag_own, diag_other, link, grad_own, grad_other)


def conjugate_steps(right_side, apply_operator, inner_product):
    solution = jnp.zeros_like(right_side)
    remainder = right_side
    direction = right_side
    norm_now = inner_product(remainder, remainder)
    for iteration in range(ITERS):
        product_vec = apply_operator(direction)
        step_size = norm_now / inner_product(direction, product_vec)
        solution = solution + step_size * direction
        remainder = remainder - step_size * product_vec
        norm_next = inner_product(remainder, remainder)
        direction = remainder + norm_next / norm_now * direction
        norm_now = norm_next
    return (solution, remainder)


def shards(cam_jac, pt_jac, resid, partner, count, tile_map):
    row_count = lax.axis_size("row")
    col_count = lax.axis_size("col")
    scenes = tile_map.shape[0]
    scn_local = partner.shape[0]
    points = partner.shape[1]
    tile_rows = scenes // row_count
    tile_cols = scenes // col_count
    per_group = scn_local // row_count
    row_index = lax.axis_index("row")
    col_index = lax.axis_index("col")
    device = row_index * col_count + col_index
    positions = jnp.arange(scenes, dtype=jnp.int32)
    tile_own = lax.dynamic_slice_in_dim(tile_map, device * scn_local, scn_local)
    local_rank = jnp.sum((tile_own[None, :] < tile_own[:, None]).astype(jnp.int32), axis=1)
    active = (jnp.arange(points, dtype=jnp.int32)[None, :] < count[:, None]).astype(jnp.float32)
    diag_own, diag_other, link, grad_own, grad_other = point_terms(cam_jac, pt_jac, resid)
    values = (
        jnp.concatenate(
            [
                link.reshape(36, scn_local, points),
                diag_other.reshape(36, scn_local, points),
                grad_other,
            ],
            axis=0,
        )
        * active[None]
    )
    values = jnp.moveaxis(values, 1, 0)

    def scene_sums(item):
        scene_values, scene_partner = item
        hits = scene_partner[:, None] == positions[None, :]
        tile_other = jnp.sum(jnp.where(hits, tile_map[None, :], 0), axis=1)
        onehot = (tile_other[:, None] == positions[None, :]).astype(jnp.float32)
        return jnp.dot(
            scene_values,
            onehot,
            precision=lax.Precision.HIGHEST,
            preferred_element_type=jnp.float32,
        )

    per_scene = lax.map(scene_sums, (values, partner))
    link_rows = per_scene[:, :36, :]
    other_sum = jnp.sum(per_scene[:, 36:, :], axis=0)
    ordering = (local_rank[None, :] == jnp.arange(scn_local, dtype=jnp.int32)[:, None]).astype(
        jnp.float32
    )
    panel = jnp.einsum("rs,sxc->xrc", ordering, link_rows, precision=lax.Precision.HIGHEST)
    panel = panel.reshape(36, row_count, per_group, col_count, tile_cols).transpose(0, 1, 3, 2, 4)
    panel_short = panel.astype(jnp.bfloat16)
    own_onehot = (tile_own[:, None] == positions[None, :]).astype(jnp.float32)
    own_diag = jnp.sum(diag_own * active, axis=-1).reshape(36, scn_local)
    own_grad = jnp.sum(grad_own * active, axis=-1)
    own_both = jnp.concatenate([own_diag, own_grad], axis=0)
    own_spread = jnp.dot(
        own_both, own_onehot, precision=lax.Precision.HIGHEST, preferred_element_type=jnp.float32
    )
    both_part = own_spread + other_sum
    diag_part = both_part[:36]
    grad_part = both_part[36:]
    shaped = panel_short.reshape(36, row_count * col_count, per_group, tile_cols)
    received = lax.all_to_all(shaped, ("row", "col"), split_axis=1, concat_axis=1, tiled=True)
    received = received.reshape(36, tile_rows, tile_cols)
    diag_all, grad_all = lax.psum((diag_part, grad_part), ("row", "col"))
    row_start = row_index * tile_rows
    col_start = col_index * tile_cols
    devices = scenes // scn_local
    tiles_grid = tile_map.reshape(devices, scn_local)
    inblock = (tiles_grid >= row_start) & (tiles_grid < row_start + tile_rows)
    lower = (tiles_grid[:, None, :] < tiles_grid[:, :, None]) & inblock[:, None, :]
    within_all = jnp.sum(lower.astype(jnp.int32), axis=2)
    slot_from = (jnp.arange(devices, dtype=jnp.int32)[:, None] * per_group + within_all).reshape(-1)
    slot_to = (tiles_grid - row_start).reshape(-1)
    slots = jnp.arange(tile_rows, dtype=jnp.int32)
    to_table = ((slot_to[:, None] == slots[None, :]) & inblock.reshape(-1)[:, None]).astype(
        jnp.bfloat16
    )
    from_table = (slot_from[:, None] == slots[None, :]).astype(jnp.bfloat16)
    selection = jnp.dot(to_table.T, from_table, preferred_element_type=jnp.float32).astype(
        jnp.bfloat16
    )
    coupling_tile = jnp.einsum(
        "pk,xkc->xpc", selection, received, preferred_element_type=jnp.float32
    )
    coupling_tile = coupling_tile.astype(jnp.bfloat16).reshape(6, 6, tile_rows, tile_cols)
    coupling_wide = coupling_tile.astype(jnp.float32)
    zero_at = row_index * 0

    def tile_products(rows_part, cols_part):
        forward = jnp.einsum(
            "xyij,yj->xi", coupling_wide, cols_part, precision=lax.Precision.HIGHEST
        )
        backward = jnp.einsum(
            "xyij,xi->yj", coupling_wide, rows_part, precision=lax.Precision.HIGHEST
        )
        empty = jnp.zeros((6, scenes), jnp.float32)
        spread = lax.dynamic_update_slice(empty, forward, (zero_at, row_start))
        spread = spread + lax.dynamic_update_slice(empty, backward, (zero_at, col_start))
        return lax.psum(spread, ("row", "col"))

    diag_blocks = diag_all.reshape(6, 6, scenes)

    def apply_full(direction):
        rows_part = lax.dynamic_slice_in_dim(direction, row_start, tile_rows, 1)
        cols_part = lax.dynamic_slice_in_dim(direction, col_start, tile_cols, 1)
        summed = tile_products(rows_part, cols_part)
        result = CAMERA_DAMPING * direction
        result = result + jnp.einsum(
            "xyi,yi->xi", diag_blocks, direction, precision=lax.Precision.HIGHEST
        )
        return result + summed

    def inner_full(first_vec, second_vec):
        return jnp.sum(first_vec * second_vec)

    whole_solution, whole_remainder = conjugate_steps(grad_all, apply_full, inner_full)
    solution = lax.dynamic_slice_in_dim(whole_solution, row_start, tile_rows, 1)
    remainder = lax.dynamic_slice_in_dim(whole_remainder, row_start, tile_rows, 1)
    return (coupling_tile, solution, remainder)


def solution(mesh):
    return jax.shard_map(
        shards,
        mesh=mesh,
        in_specs=(
            P(None, None, None, ("row", "col"), None),
            P(None, None, None, ("row", "col"), None),
            P(None, None, ("row", "col"), None),
            P(("row", "col"), None),
            P(("row", "col")),
            P(),
        ),
        out_specs=(P(None, None, "row", "col"), P(None, "row"), P(None, "row")),
        check_vma=False,
    )
```

profile of v0, /device:TPU:1, one launch (start us, length us, event | category | flops | bytes accessed | tf_op | source)
XLA Modules:
  0.0 580.1 jit_solution(9334390753709633188)
XLA Ops:
  20.8 4.8 multiply_reduce_fusion
  31.1 131.4 %while.12 = (s32[]{:T(128)}, f32[16,78,2048]{2,1,0:T(8,128)}, f32[16,78,1024]{2,0,1:T(8,128)}, s32[16,1024]{1,0:T(8,128)}, s32[2048]{0:T(1024)S(1)}, /*index=5*/s32[]{:T(128)}) while((s32[]{:T(128)}, f32[16,78,2048]{2,1,0:T(8,128)}, f32[16,78,1024]{2,0,1:T(8,128)}, s32[16,1024]{1,0:T(8,128)}, s32[2048]{0:T(1024)S(1)}, ...), condition=%wide.region_16.0_spmd.clone.clone, body=%wide.region_14.16_spmd.clone.clone.sunk | while | flops 1971321856 | bytes 1642585 | solution.py:124
  43.4 4.1 fusion.70
  51.6 4.2 fusion.70
  59.8 4.1 fusion.70
  68.0 4.1 fusion.70
  76.2 4.1 fusion.70
  92.6 4.1 fusion.70
  100.8 4.1 fusion.70
  109.0 4.1 fusion.70
  117.2 4.1 fusion.70
  125.4 4.1 fusion.70
  133.6 4.2 fusion.70
  141.8 4.2 fusion.70
  150.0 4.1 fusion.70
  158.2 4.1 fusion.70
  162.5 7.6 %fusion.9 = bf16[36,2048,16]{1,2,0:T(8,128)(2,1)S(1)} fusion(f32[16,78,2048]{2,1,0:T(8,128)} %get-tuple-element.38, s32[16]{0:T(128)S(1)} %convert_reduce_fusion.1), kind=kOutput, calls=%fused_computation.23 | convolution fusion | flops 227672320 | bytes 12582976 | tf_op jit(solution)/shard_map/rs,sxc->xrc/dot_general | solution.py:130
  175.3 11.5 %all-to-all-start = ((bf16[36,128,2,128]{3,2,0,1:T(2,128)(2,1)}), bf16[36,128,2,128]{3,2,0,1:T(2,128)(2,1)S(1)}, u32[]{:S(2)}, u32[]{:S(2)}) async-start(bf16[36,128,2,128]{3,2,0,1:T(2,128)(2,1)} %copy.49), calls=%async_computation | async-start | bytes 4718592 | tf_op jit(solution)/shard_map/all_to_all | solution.py:144
  195.0 77.2 %psum.35 = f32[6,2048]{1,0:T(8,128)S(1)} all-reduce(f32[6,2048]{1,0:T(8,128)S(1)} %slice.143), channel_id=1, replica_groups=mesh['row'=8,'col'=16] {'row','col'}, use_global_device_ids=true, to_apply=%region_26.27 | all-reduce | flops 12288 | bytes 98304 | tf_op jit(solution)/shard_map/psum | solution.py:146
  272.5 77.3 %all-reduce.2.cloned.1.call-done = f32[6,6,2048]{2,1,0:T(8,128)} async-done(((f32[6,6,2048]{2,1,0:T(8,128)}), f32[6,6,2048]{2,1,0:T(8,128)}) %all-reduce.2.cloned.1.call-update) | async-done | bytes 294928 | tf_op jit(solution)/shard_map/psum | solution.py:146
  354.8 4.3 convolution_convert_fusion
  362.1 63.9 %psum.37 = f32[6,2048]{1,0:T(8,128)S(1)} all-reduce(f32[6,2048]{1,0:T(8,128)S(1)} %constant_dynamic-update-slice_fusion.2), channel_id=1, replica_groups=mesh['row'=8,'col'=16] {'row','col'}, use_global_device_ids=true, to_apply=%region_29.30 | all-reduce | flops 12288 | bytes 98304 | tf_op jit(solution)/shard_map/psum | solution.py:181
  433.0 64.3 %psum.38 = f32[6,2048]{1,0:T(8,128)S(1)} all-reduce(f32[6,2048]{1,0:T(8,128)S(1)} %constant_dynamic-update-slice_fusion.1), channel_id=1, replica_groups=mesh['row'=8,'col'=16] {'row','col'}, use_global_device_ids=true, to_apply=%region_32.33 | all-reduce | flops 12288 | bytes 98304 | tf_op jit(solution)/shard_map/psum | solution.py:181
  506.8 62.7 %psum.39 = f32[6,2048]{1,0:T(8,128)S(1)} all-reduce(f32[6,2048]{1,0:T(8,128)S(1)} %constant_dynamic-update-slice_fusion), channel_id=1, replica_groups=mesh['row'=8,'col'=16] {'row','col'}, use_global_device_ids=true, to_apply=%region_35.36 | all-reduce | flops 12288 | bytes 98304 | tf_op jit(solution)/shard_map/psum | solution.py:181
  (159 shorter events, 126.6 us)
Async XLA Ops:
  8.5 1.6 copy-start.4
  8.5 1.6 copy-start.3
  12.8 2.7 copy-start.5
  12.8 3.5 copy-start.6
  15.6 0.5 copy-start.7
  26.0 1.0 copy-start.2
  26.0 1.8 copy-start
  175.3 175.6 %all-to-all-start = ((bf16[36,128,2,128]{3,2,0,1:T(2,128)(2,1)}), bf16[36,128,2,128]{3,2,0,1:T(2,128)(2,1)S(1)}, u32[]{:S(2)}, u32[]{:S(2)}) async-start(bf16[36,128,2,128]{3,2,0,1:T(2,128)(2,1)} %copy.49), calls=%async_computation | async-start | bytes 4718592 | tf_op jit(solution)/shard_map/all_to_all | solution.py:144
  186.8 162.9 %all-reduce.2.cloned.1.call-start = ((), (), s32[]{:S(2)}) async-start(), calls=%async_computation.1 | async-start | bytes 786432 | tf_op jit(solution)/shard_map/psum | solution.py:146
  189.8 3.7 copy-start.8
  430.0 67.3 %copy-start.1 = (f32[6,6,2048]{2,1,0:T(8,128)S(1)}, f32[6,6,2048]{2,1,0:T(8,128)}, u32[]{:S(2)}) copy-start(f32[6,6,2048]{2,1,0:T(8,128)} %all-reduce.2.cloned.1.call-done) | copy-start | bytes 884740
Sparse Core Ops, SparseCore 0:
  194.9 154.7 all-reduce.1
where the time goes:
time: 591 us; the launch traced here: 580 us
  blocking collectives  268 us (45%)
  matrix products  87.4 us (15%)
  waiting for transfers between devices  77.3 us (13%)
  local copies, waits for them, and re-layouts  59.7 us (10%)
  other arithmetic  54.1 us (9%)
  between operations  21.6 us (4%)
  starting transfers between devices  11.5 us (2%)
    psum x3, blocking collectives, tile_products(): return lax.psum(spread, ('row', 'col'))  191 us
    psum x1, waiting for transfers between devices, shards(): diag_all, grad_all = lax.psum((diag_part, grad_part), ('row', 'col'))  77.3 us
    psum x1, blocking collectives, shards(): diag_all, grad_all = lax.psum((diag_part, grad_part), ('row', 'col'))  77.2 us
    dot_general x16, matrix products, scene_sums(): jnp.dot(scene_values, onehot, precision=lax.Precision.HIGHEST, preferred_...  66.2 us
    dynamic_slice x32, local copies, waits for them, and re-layouts, shards(): per_scene = lax.map(scene_sums, (values, partner))  44.5 us
    reduce_sum x16, other arithmetic, scene_sums(): tile_other = jnp.sum(jnp.where(hits, tile_map[None, :], 0), axis=1)  20.3 us
  transfers between devices with their start and end apart: 2, of which 1 were waited for; matrix products, arithmetic and copies ran while one was open for 2% of the time, Pallas kernels for 0%

commit v1 on v0

v1 whole, which is shorter than its diff:
```python
import functools

import jax
import jax.numpy as jnp
from jax import lax
from jax.experimental import pallas as pl
from jax.experimental.pallas import tpu as pltpu
from jax.sharding import PartitionSpec as P

ITERS = 3
CAMERA_DAMPING = 1.0
POINT_DAMPING = 1.0

F32 = jnp.float32
BF16 = jnp.bfloat16
MESH = pl.DeviceIdType.MESH
LANES = 128

LINK = 36
PAIRS = [(x, y) for x in range(6) for y in range(x, 6)]
DIAG = len(PAIRS)
VALUES = 64
GRAD_AT = 24
SUM_ROWS = 32


def pair_index(x, y):
    return PAIRS.index((min(x, y), max(x, y)))


def dot3(first, second):
    total = first[0] * second[0]
    for k in range(1, len(first)):
        total = total + first[k] * second[k]
    return total


def point_chunk(cam_ref, pt_ref, res_ref, active, at):
    def cam(side, i):
        return [cam_ref[side, i, x, :, at].astype(F32) for x in range(6)]

    pa = [[pt_ref[0, i, k, :, at].astype(F32) for k in range(3)] for i in range(2)]
    pb = [[pt_ref[1, i, k, :, at].astype(F32) for k in range(3)] for i in range(2)]
    ea = [res_ref[0, i, :, at].astype(F32) for i in range(2)]
    eb = [res_ref[1, i, :, at].astype(F32) for i in range(2)]

    def hess(m, n):
        return pa[0][m] * pa[0][n] + pa[1][m] * pa[1][n] + (pb[0][m] * pb[0][n] + pb[1][m] * pb[1][n])

    v00, v11, v22 = (hess(k, k) + POINT_DAMPING for k in range(3))
    v01, v02, v12 = hess(0, 1), hess(0, 2), hess(1, 2)
    c00 = v11 * v22 - v12 * v12
    c01 = v02 * v12 - v01 * v22
    c02 = v01 * v12 - v02 * v11
    c11 = v00 * v22 - v02 * v02
    c12 = v01 * v02 - v00 * v12
    c22 = v00 * v11 - v01 * v01
    det = v00 * c00 + v01 * c01 + v02 * c02
    scale = 1.0 / det
    i00, i01, i02 = c00 * scale, c01 * scale, c02 * scale
    i11, i12, i22 = c11 * scale, c12 * scale, c22 * scale
    inv = [[i00, i01, i02], [i01, i11, i12], [i02, i12, i22]]
    q = [-(pa[0][k] * ea[0] + pa[1][k] * ea[1] + (pb[0][k] * eb[0] + pb[1][k] * eb[1])) for k in range(3)]
    pav = [[dot3(pa[i], inv[k]) for k in range(3)] for i in range(2)]
    pbv = [[dot3(pb[i], inv[k]) for k in range(3)] for i in range(2)]

    def schur(pv, p):
        n00 = (1.0 - dot3(pv[0], p[0])) * active
        n01 = -dot3(pv[0], p[1]) * active
        n11 = (1.0 - dot3(pv[1], p[1])) * active
        return [[n00, n01], [n01, n11]]

    naa, nbb = schur(pav, pa), schur(pbv, pb)
    mab = [[-dot3(pav[i], pb[j]) * active for j in range(2)] for i in range(2)]
    ga = [-(ea[i] + dot3(pav[i], q)) * active for i in range(2)]
    gb = [-(eb[i] + dot3(pbv[i], q)) * active for i in range(2)]
    ja = [cam(0, 0), cam(0, 1)]
    jb = [cam(1, 0), cam(1, 1)]

    def quad(left, middle, right, pairs):
        half = [[middle[i][0] * right[0][y] + middle[i][1] * right[1][y] for y in range(6)] for i in range(2)]
        return [left[0][x] * half[0][y] + left[1][x] * half[1][y] for x, y in pairs]

    link = quad(ja, mab, jb, [(x, y) for x in range(6) for y in range(6)])
    diag_other = quad(jb, nbb, jb, PAIRS)
    grad_other = [jb[0][x] * gb[0] + jb[1][x] * gb[1] for x in range(6)]
    diag_own = quad(ja, naa, ja, PAIRS)
    grad_own = [ja[0][x] * ga[0] + ja[1][x] * ga[1] for x in range(6)]
    return link + diag_other + grad_other, diag_own + grad_own


def assemble_kernel(
    own_ref, cam_ref, pt_ref, res_ref, partner_ref, count_ref, map_ref, own_col_ref,
    panel_ref, sums_ref,
    high, low, own_acc, lane_index, group_index, lhs, acc, weave, order,
):
    step = pl.program_id(0)
    scn, points = partner_ref.shape
    chunks = points // LANES
    scenes = map_ref.shape[0] * LANES
    groups = scenes // 256

    @pl.when(step == 0)
    def _():
        for s in range(scn):
            rank = jnp.int32(0)
            for t in range(scn):
                if t != s:
                    rank = rank + (own_ref[t] < own_ref[s]).astype(jnp.int32)
            order[rank] = jnp.int32(s)
        own_acc[...] = jnp.zeros_like(own_acc)
        acc[...] = jnp.zeros_like(acc)
        high[pl.ds((VALUES - 1) * scn, scn), :] = jnp.zeros((scn, points), F32)
        low[pl.ds((VALUES - 1) * scn, scn), :] = jnp.zeros((scn, points), F32)

        @pl.loop(0, chunks)
        def _(j):
            at = pl.ds(pl.multiple_of(j * LANES, LANES), LANES)
            slot = lax.broadcasted_iota(jnp.int32, (scn, LANES), 1) + j * LANES
            active = (slot < count_ref[...]).astype(F32)
            values, own = point_chunk(cam_ref, pt_ref, res_ref, active, at)
            for v, value in enumerate(values):
                top = value.astype(BF16).astype(F32)
                high[pl.ds(v * scn, scn), at] = top
                low[pl.ds(v * scn, scn), at] = value - top
            for v, value in enumerate(own):
                own_acc[v] += value
            partner = partner_ref[:, at]
            which = partner & (LANES - 1)
            line = partner >> 7
            tile = jnp.zeros((scn, LANES), jnp.int32)
            for h in range(map_ref.shape[0]):
                row = jnp.broadcast_to(map_ref[h : h + 1, :], (scn, LANES))
                tile = jnp.where(line == h, jnp.take_along_axis(row, which, axis=1), tile)
            column = tile >> 7
            lane_index[:, at] = ((column >> 3) << 7) | (tile & (LANES - 1))
            group_index[:, at] = column & 7

    for slot in range(2):
        s = order[step * 2 + slot]
        group_row = jnp.broadcast_to(group_index[pl.ds(s, 1), :], (groups, points))
        keep = group_row == lax.broadcasted_iota(jnp.int32, (groups, points), 0)
        lane_row = lane_index[pl.ds(s, 1), :]
        onehot = jnp.where(
            lane_row == lax.broadcasted_iota(jnp.int32, (256, points), 0), 1.0, 0.0
        ).astype(BF16)
        for part, source in enumerate((high, low)):
            for v in range(0, VALUES, 2):
                rows = [
                    jnp.where(keep, jnp.broadcast_to(source[pl.ds((v + k) * scn + s, 1), :], (groups, points)), 0.0)
                    for k in range(2)
                ]
                lhs[pl.ds((part * VALUES + v) * groups, 2 * groups), :] = jnp.concatenate(rows, axis=0).astype(BF16)
        result = lax.dot_general(
            lhs[...], onehot, (((1,), (1,)), ((), ())), preferred_element_type=F32
        )
        result = result[: VALUES * groups] + result[VALUES * groups :]
        for x in range(LINK):
            for b in range(2):
                weave[pl.ds((x * 2 + b) * 2 * groups + slot, groups, stride=2), :] = result[
                    x * groups : (x + 1) * groups, b * LANES : (b + 1) * LANES
                ]
        for b in range(2):
            acc[pl.ds(b * (VALUES - LINK) * groups, (VALUES - LINK) * groups), :] += result[
                LINK * groups :, b * LANES : (b + 1) * LANES
            ]
    panel_ref[...] = weave[...].reshape(LINK, 1, 2, 2 * groups, LANES).astype(BF16)

    @pl.when(step == pl.num_programs(0) - 1)
    def _():
        lanes = lax.broadcasted_iota(jnp.int32, (scn, LANES), 1)
        own_table = jnp.zeros((scn, LANES), F32)
        for v in range(DIAG + 6):
            total = jnp.sum(own_acc[v], axis=1, keepdims=True)
            own_table = jnp.where(lanes == (v if v < DIAG else GRAD_AT + v - DIAG), total, own_table)
        spread = (own_col_ref[...] == lax.broadcasted_iota(jnp.int32, (scn, scenes), 1)).astype(F32)
        own_sum = lax.dot_general(
            own_table.T[:SUM_ROWS], spread, (((1,), (0,)), ((), ())),
            precision=lax.Precision.HIGHEST, preferred_element_type=F32,
        )
        zeros = jnp.zeros((3, LANES), F32)
        for b in range(2):
            for h in range(groups):
                column = b * groups + h
                other = acc[pl.ds(b * (VALUES - LINK) * groups + h, VALUES - LINK, stride=groups), :]
                whole = jnp.concatenate(
                    [other[:DIAG], zeros, other[DIAG : DIAG + 6], zeros[:2]], axis=0
                )
                sums_ref[column // 2, :, (column % 2) * LANES : (column % 2 + 1) * LANES] = (
                    whole + own_sum[:, column * LANES : (column + 1) * LANES]
                )


def assemble(cam_jac, pt_jac, resid, partner, count, tile_map, tile_own):
    scn, points = partner.shape
    scenes = tile_map.shape[0]
    groups = scenes // 256
    rows = scenes // 256
    whole = lambda shape: pl.BlockSpec(shape, lambda i: (0,) * len(shape))
    map2 = tile_map.reshape(scenes // LANES, LANES)
    return pl.pallas_call(
        assemble_kernel,
        grid=(rows,),
        in_specs=[
            pl.BlockSpec(memory_space=pltpu.SMEM),
            whole(cam_jac.shape),
            whole(pt_jac.shape),
            whole(resid.shape),
            whole(partner.shape),
            whole((scn, 1)),
            whole(map2.shape),
            whole((scn, 1)),
        ],
        out_specs=[
            pl.BlockSpec((LINK, 1, 2, 2 * groups, LANES), lambda i: (0, i, 0, 0, 0)),
            whole((rows, SUM_ROWS, 256)),
        ],
        out_shape=[
            jax.ShapeDtypeStruct((LINK, rows, 2, 2 * groups, LANES), BF16),
            jax.ShapeDtypeStruct((rows, SUM_ROWS, 256), F32),
        ],
        scratch_shapes=[
            pltpu.VMEM((VALUES * scn, points), F32),
            pltpu.VMEM((VALUES * scn, points), F32),
            pltpu.VMEM((DIAG + 6, scn, LANES), F32),
            pltpu.VMEM((scn, points), jnp.int32),
            pltpu.VMEM((scn, points), jnp.int32),
            pltpu.VMEM((2 * VALUES * groups, points), BF16),
            pltpu.VMEM((2 * (VALUES - LINK) * groups, LANES), F32),
            pltpu.VMEM((LINK * 2 * 2 * groups, LANES), F32),
            pltpu.SMEM((scn,), jnp.int32),
        ],
        compiler_params=pltpu.CompilerParams(
            dimension_semantics=("arbitrary",), vmem_limit_bytes=48 * 1024 * 1024
        ),
        name="assemble",
    )(tile_own, cam_jac, pt_jac, resid, partner, count.reshape(scn, 1), map2, tile_own.reshape(scn, 1))


def select_kernel(tiles_ref, received_ref, out_ref, selection):
    row_start = lax.axis_index("row") * 256

    @pl.when(pl.program_id(0) == 0)
    def _():
        offset = tiles_ref[...] - row_start
        inside = (offset >= 0) & (offset < 256)
        least = jnp.min(jnp.where(inside, offset, 256), axis=0, keepdims=True)
        most = jnp.max(jnp.where(inside, offset, -1), axis=0, keepdims=True)
        odd = lax.broadcasted_iota(jnp.int32, least.shape, 1) & 1
        position = jnp.where(odd == 0, least, most)
        slots = position.shape[1]
        selection[...] = jnp.where(
            position == lax.broadcasted_iota(jnp.int32, (256, slots), 0), 1.0, 0.0
        ).astype(BF16)

    for k in range(received_ref.shape[0]):
        out_ref[k] = jnp.dot(selection[...], received_ref[k], preferred_element_type=F32).astype(BF16)


def select_rows(tile_map, received, scn):
    devices = tile_map.shape[0] // scn
    tiles = jnp.repeat(tile_map.reshape(devices, scn).T, 2, axis=1)
    block = 6
    return pl.pallas_call(
        select_kernel,
        grid=(LINK // block,),
        in_specs=[
            pl.BlockSpec(tiles.shape, lambda i: (0, 0)),
            pl.BlockSpec((block, 256, LANES), lambda i: (i, 0, 0)),
        ],
        out_specs=pl.BlockSpec((block, 256, LANES), lambda i: (i, 0, 0)),
        out_shape=jax.ShapeDtypeStruct((LINK, 256, LANES), BF16),
        scratch_shapes=[pltpu.VMEM((256, 2 * devices), BF16)],
        compiler_params=pltpu.CompilerParams(dimension_semantics=("arbitrary",)),
        name="select_rows",
    )(tiles, received)


def spread_along(axis, n, buffer, send, recv):
    me = lax.axis_index(axis)
    copies = []
    for k in range(1, n):
        there = lax.rem(me + k, n)
        copy = pltpu.make_async_remote_copy(
            src_ref=buffer.at[me],
            dst_ref=buffer.at[me],
            send_sem=send.at[k],
            recv_sem=recv.at[k],
            device_id={axis: there},
            device_id_type=MESH,
        )
        copy.start()
        copies.append(copy)
    return copies


def enter(rows, cols):
    barrier = pltpu.get_barrier_semaphore()
    for axis, n in (("row", rows), ("col", cols)):
        me = lax.axis_index(axis)
        for k in range(1, n):
            pl.semaphore_signal(barrier, inc=1, device_id={axis: lax.rem(me + k, n)}, device_id_type=MESH)
    pl.semaphore_wait(barrier, rows + cols - 2)


def slot_sum(buffer):
    total = buffer[0]
    for k in range(1, buffer.shape[0]):
        total = total + buffer[k]
    return total


def diagonal_kernel(
    rows, cols, sums_ref, blocks_ref, right_ref, parts, first, second,
    send_parts, recv_parts, send_first, recv_first, send_second, recv_second,
):
    row, col = lax.axis_index("row"), lax.axis_index("col")
    enter(rows, cols)
    copies = []
    for k in range(1, rows):
        there = lax.rem(row + k, rows)
        copy = pltpu.make_async_remote_copy(
            src_ref=sums_ref.at[there],
            dst_ref=parts.at[row],
            send_sem=send_parts.at[k],
            recv_sem=recv_parts.at[k],
            device_id={"row": there},
            device_id_type=MESH,
        )
        copy.start()
        copies.append(copy)
    parts[row] = sums_ref[row]
    for copy in copies:
        copy.wait()
    total = slot_sum(parts)
    first[col] = total[GRAD_AT : GRAD_AT + 8]
    copies = spread_along("col", cols, first, send_first, recv_first)
    line = lax.broadcasted_iota(jnp.int32, (8, 256), 0)
    for y in range(6):
        block = jnp.zeros((8, 256), F32)
        for x in range(6):
            v = pair_index(x, y)
            block = jnp.where(line == x, jnp.broadcast_to(total[v : v + 1], (8, 256)), block)
        blocks_ref[y] = block
    for copy in copies:
        copy.wait()
    second[row] = slot_sum(first)
    for copy in spread_along("row", rows, second, send_second, recv_second):
        copy.wait()
    right_ref[...] = second[...]


def add_diagonals(sums, rows, cols):
    return pl.pallas_call(
        functools.partial(diagonal_kernel, rows, cols),
        in_specs=[pl.BlockSpec(memory_space=pltpu.VMEM)],
        out_specs=[pl.BlockSpec(memory_space=pltpu.VMEM)] * 2,
        out_shape=[
            jax.ShapeDtypeStruct((6, 8, 256), F32),
            jax.ShapeDtypeStruct((rows, 8, 256), F32),
        ],
        scratch_shapes=[
            pltpu.VMEM((rows, SUM_ROWS, 256), F32),
            pltpu.VMEM((cols, 8, 256), F32),
            pltpu.VMEM((rows, 8, 256), F32),
            pltpu.SemaphoreType.DMA((rows,)),
            pltpu.SemaphoreType.DMA((rows,)),
            pltpu.SemaphoreType.DMA((cols,)),
            pltpu.SemaphoreType.DMA((cols,)),
            pltpu.SemaphoreType.DMA((rows,)),
            pltpu.SemaphoreType.DMA((rows,)),
        ],
        compiler_params=pltpu.CompilerParams(collective_id=1, has_side_effects=True),
        cost_estimate=pl.CostEstimate(flops=40_000_000, bytes_accessed=1_000_000, transcendentals=0),
        name="add_diagonals",
    )(sums)


def three_terms(value):
    first = value.astype(BF16)
    rest = value - first.astype(F32)
    second = rest.astype(BF16)
    third = (rest - second.astype(F32)).astype(BF16)
    return jnp.concatenate([first.astype(F32), second.astype(F32), third.astype(F32)], axis=0)


def row_masked(stacked, which):
    line = lax.broadcasted_iota(jnp.int32, stacked.shape, 0) & 7
    return jnp.where(line == which, stacked, 0.0).astype(BF16)


def conjugate_kernel(
    rows, cols, tile_ref, blocks_ref, right_ref, update_ref, residual_ref,
    direction, remainder, answer, row_firsts, col_first, row_second, col_seconds,
    send_row, recv_row, send_col, recv_col, send_row2, recv_row2, send_col2, recv_col2,
):
    row, col = lax.axis_index("row"), lax.axis_index("col")
    enter(rows, cols)
    direction[...] = right_ref[...]
    remainder[...] = right_ref[...]
    answer[...] = jnp.zeros_like(answer)

    def inner(first, second):
        total = first[0] * second[0]
        for r in range(1, rows):
            total = total + first[r] * second[r]
        return jnp.sum(jnp.sum(total, axis=0, keepdims=True), axis=1, keepdims=True)

    start = right_ref[...]
    norm_now = inner(start, start)

    def iteration(step, norm_now):
        parity = lax.rem(step, 2)
        row_first, col_second = row_firsts.at[parity], col_seconds.at[parity]
        rows_part = direction[row]
        cols_part = direction[col // 2, :, pl.ds(pl.multiple_of((col % 2) * LANES, LANES), LANES)]
        row_terms, col_terms = three_terms(rows_part), three_terms(cols_part)
        col_lhs = [row_masked(col_terms, y) for y in range(6)]
        row_lhs = [row_masked(row_terms, x) for x in range(6)]
        line_rows = lax.broadcasted_iota(jnp.int32, (8, 256), 0)
        line_cols = lax.broadcasted_iota(jnp.int32, (8, LANES), 0)
        forward = jnp.zeros((8, 256), F32)
        for y in range(6):
            forward = forward + blocks_ref[y] * jnp.broadcast_to(rows_part[y : y + 1], (8, 256))
        for x in range(6):
            total = None
            for y in range(6):
                part = lax.dot_general(
                    col_lhs[y], tile_ref[x * 6 + y], (((1,), (1,)), ((), ())), preferred_element_type=F32
                )
                total = part if total is None else total + part
            forward = forward + jnp.where(line_rows == x, jnp.sum(total, axis=0, keepdims=True), 0.0)
        row_first[col] = forward
        copies = spread_along("col", cols, row_first, send_row.at[parity], recv_row.at[parity])
        backward = jnp.zeros((8, LANES), F32)
        for y in range(6):
            total = None
            for x in range(6):
                part = jnp.dot(row_lhs[x], tile_ref[x * 6 + y], preferred_element_type=F32)
                total = part if total is None else total + part
            backward = backward + jnp.where(line_cols == y, jnp.sum(total, axis=0, keepdims=True), 0.0)
        col_first[row] = backward
        copies_col = spread_along("row", rows, col_first, send_col, recv_col)
        for copy in copies_col:
            copy.wait()
        col_second[col] = slot_sum(col_first)
        second_copies = spread_along("col", cols, col_second, send_col2.at[parity], recv_col2.at[parity])
        for copy in copies:
            copy.wait()
        row_second[row] = slot_sum(row_first)
        for copy in spread_along("row", rows, row_second, send_row2, recv_row2):
            copy.wait()
        for copy in second_copies:
            copy.wait()
        held = direction[...]
        image = CAMERA_DAMPING * held + row_second[...]
        back = jnp.stack(
            [jnp.concatenate([col_second[2 * r], col_second[2 * r + 1]], axis=1) for r in range(rows)], axis=0
        )
        image = image + back
        step_size = norm_now / inner(held, image)
        answer[...] = answer[...] + step_size[None] * held
        left = remainder[...] - step_size[None] * image
        remainder[...] = left
        norm_next = inner(left, left)
        direction[...] = left + (norm_next / norm_now)[None] * held
        return norm_next

    lax.fori_loop(0, ITERS, iteration, norm_now)
    update_ref[...] = answer[row][:6]
    residual_ref[...] = remainder[row][:6]


def conjugate(tile, blocks, right, rows, cols):
    dma = pltpu.SemaphoreType.DMA
    return pl.pallas_call(
        functools.partial(conjugate_kernel, rows, cols),
        in_specs=[pl.BlockSpec(memory_space=pltpu.VMEM)] * 3,
        out_specs=[pl.BlockSpec(memory_space=pltpu.VMEM)] * 2,
        out_shape=[jax.ShapeDtypeStruct((6, 256), F32)] * 2,
        scratch_shapes=[
            pltpu.VMEM((rows, 8, 256), F32),
            pltpu.VMEM((rows, 8, 256), F32),
            pltpu.VMEM((rows, 8, 256), F32),
            pltpu.VMEM((2, cols, 8, 256), F32),
            pltpu.VMEM((rows, 8, LANES), F32),
            pltpu.VMEM((rows, 8, 256), F32),
            pltpu.VMEM((2, cols, 8, LANES), F32),
            dma((2, cols)), dma((2, cols)), dma((rows,)), dma((rows,)),
            dma((rows,)), dma((rows,)), dma((2, cols)), dma((2, cols)),
        ],
        compiler_params=pltpu.CompilerParams(collective_id=2, has_side_effects=True),
        name="conjugate",
    )(tile, blocks, right)


def shards(cam_jac, pt_jac, resid, partner, count, tile_map):
    rows, cols = lax.axis_size("row"), lax.axis_size("col")
    scn = partner.shape[0]
    device = lax.axis_index("row") * cols + lax.axis_index("col")
    tile_own = lax.dynamic_slice_in_dim(tile_map, device * scn, scn)
    panel, sums = assemble(cam_jac, pt_jac, resid, partner, count, tile_map, tile_own)
    shaped = panel.reshape(LINK, rows * cols, 2, LANES)
    received = lax.all_to_all(shaped, ("row", "col"), split_axis=1, concat_axis=1, tiled=True)
    blocks, right = add_diagonals(sums, rows, cols)
    tile = select_rows(tile_map, received.reshape(LINK, 256, LANES), scn)
    update, residual = conjugate(tile, blocks, right, rows, cols)
    return tile.reshape(6, 6, 256, LANES), update, residual


def solution(mesh):
    return jax.shard_map(
        shards,
        mesh=mesh,
        in_specs=(
            P(None, None, None, ("row", "col"), None),
            P(None, None, None, ("row", "col"), None),
            P(None, None, ("row", "col"), None),
            P(("row", "col"), None),
            P(("row", "col")),
            P(),
        ),
        out_specs=(P(None, None, "row", "col"), P(None, "row"), P(None, "row")),
        check_vma=False,
    )
```

time: 591 us -> 136 us (0.23); the launches traced: 580 us -> 136 us
  blocking collectives: 268 us -> 0 us
  Pallas kernels: 0 us -> 105 us
  matrix products: 87.4 us -> 0 us
  waiting for transfers between devices: 77.3 us -> 0.01 us
  other arithmetic: 54.1 us -> 0 us
  local copies, waits for them, and re-layouts: 59.7 us -> 18 us
  between operations: 21.6 us -> 0.72 us
    psum x4 -> x0, blocking collectives: 268 us -> none  [the longest x3 191 us: tile_products(): return lax.psum(spread, ('row', 'col'))]
    pallas_call x0 -> x4, Pallas kernels: none -> 105 us  [the longest x1 42.9 us: add_diagonals(): pl.pallas_call(functools.partial(diagonal_kernel, rows, cols), in_specs=[...]
    dot_general x25 -> x0, matrix products: 87.4 us -> none  [the longest x16 66.2 us: scene_sums(): jnp.dot(scene_values, onehot, precision=lax.Precision.HIGHEST, preferred_...]
    psum x1 -> x0, waiting for transfers between devices: 77.3 us -> none  [shards(): diag_all, grad_all = lax.psum((diag_part, grad_part), ('row', 'col'))]
    dynamic_slice x39 -> x1, local copies, waits for them, and re-layouts: 44.6 us -> 0.76 us  [shards(): tile_own = lax.dynamic_slice_in_dim(tile_map, device * scn, scn)]
    reduce_sum x35 -> x0, other arithmetic: 42.1 us -> none  [the longest x16 20.3 us: scene_sums(): tile_other = jnp.sum(jnp.where(hits, tile_map[None, :], 0), axis=1)]
  transfers between devices with their start and end apart: 2 -> 1, of which waited for: 1 -> 0; matrix products, arithmetic and copies ran while one was open for 2% -> 1% of each run, Pallas kernels for 0% -> 32%
where the time goes in v1:
time: 136 us
  Pallas kernels  105 us (77%)
  local copies, waits for them, and re-layouts  18 us (13%)
  starting transfers between devices  11.5 us (8%)
    pallas_call x1, Pallas kernels, add_diagonals(): pl.pallas_call(functools.partial(diagonal_kernel, rows, cols), in_specs=[...  42.9 us
    pallas_call x1, Pallas kernels, conjugate(): pl.pallas_call(functools.partial(conjugate_kernel, rows, cols), in_specs=...  40.8 us
    pallas_call x1, Pallas kernels, assemble(): pl.pallas_call(assemble_kernel, grid=(rows,), in_specs=[pl.BlockSpec(memo...  16 us
    all_to_all x1, starting transfers between devices, shards(): lax.all_to_all(shaped, ('row', 'col'), split_axis=1, concat_axis=1, tiled...  11.5 us
    unnamed x16, local copies, waits for them, and re-layouts  7.86 us
    pallas_call x1, Pallas kernels, select_rows(): pl.pallas_call(select_kernel, grid=(LINK // block,), in_specs=[pl.BlockSp...  5.79 us
    all_to_all x1, local copies, waits for them, and re-layouts, shards(): lax.all_to_all(shaped, ('row', 'col'), split_axis=1, concat_axis=1, tiled...  3.94 us
    reshape x1, local copies, waits for them, and re-layouts, shards(): shaped = panel.reshape(LINK, rows * cols, 2, LANES)  3.02 us
  transfers between devices with their start and end apart: 1, of which 0 were waited for; matrix products, arithmetic and copies ran while one was open for 1% of the time, Pallas kernels for 32%

profile of v1, /device:TPU:1, one launch (start us, length us, event | category | flops | bytes accessed | tf_op | source)
XLA Modules:
  0.0 135.6 jit_solution(11818962966596765037)
XLA Ops:
  0.6 0.8 dynamic-slice_bitcast_fusion
  1.4 0.8 dynamic_slice.3.own_ref
  2.2 0.1 copy.15.own_col_ref
  2.2 0.7 copy.14.count_ref
  3.0 1.1 copy-done
  4.1 1.0 copy-done.1
  5.1 0.9 copy-done.3
  6.0 0.8 copy-done.4
  6.9 0.7 copy-done.5
  7.5 16.0 %assemble.1 = (bf16[36,8,2,16,128]{4,3,2,1,0:T(8,128)(2,1)S(1)}, f32[8,32,256]{2,1,0:T(8,128)S(1)}) custom-call(s32[16]{0:T(128)S(1)} %dynamic_slice.3.own_ref, bf16[2,2,6,16,1024]{4,3,2,1,0:T(8,128)(2,1)S(1)} %copy-done, bf16[2,2,3,16,1024]{4,3,2,1,0:T(8,128)(2,1)S(1)} %copy-done.1, bf16[2,2,16,1024]{3,2,1,0:T(8,128)(2,1)S(1)} %copy-done.3, ...), custom_call_target="tpu_custom_call" | custom-call | tf_op jit(solution)/shard_map/assemble/pallas_call | solution.py:201
  23.6 0.0 copy-start.2
  23.6 0.7 copy-done.2
  24.3 3.0 %copy.16 = bf16[36,128,2,128]{3,2,0,1:T(2,128)(2,1)} copy(bf16[36,128,2,128]{3,2,1,0:T(2,128)(2,1)S(1)} %bitcast.9) | data formatting | bytes 4718592 | tf_op jit(solution)/shard_map/reshape | solution.py:503
  27.3 11.5 %all-to-all-start = ((bf16[36,128,2,128]{3,2,0,1:T(2,128)(2,1)}), bf16[36,128,2,128]{3,2,0,1:T(2,128)(2,1)S(1)}, u32[]{:S(2)}, u32[]{:S(2)}) async-start(bf16[36,128,2,128]{3,2,0,1:T(2,128)(2,1)} %copy.16), calls=%async_computation | async-start | bytes 4718592 | tf_op jit(solution)/shard_map/all_to_all | solution.py:504
  38.8 0.0 copy-done.6
  38.8 0.1 reshape.30
  38.9 0.7 copy.18.tiles_ref
  39.6 42.9 %add_diagonals.1 = (f32[6,8,256]{2,1,0:T(8,128)}, f32[8,8,256]{2,1,0:T(8,128)}) custom-call(f32[8,32,256]{2,1,0:T(8,128)} %copy-done.2), custom_call_target="tpu_custom_call" | custom-call | flops 40000000 | bytes 1000000 | tf_op jit(solution)/shard_map/add_diagonals/pallas_call | solution.py:354
  82.5 0.0 all-to-all-done
  82.5 3.9 %copy.17 = bf16[36,128,2,128]{3,2,1,0:T(2,128)(2,1)} copy(bf16[36,128,2,128]{3,2,0,1:T(2,128)(2,1)S(1)} %all-to-all-done) | data formatting | bytes 4718592 | tf_op jit(solution)/shard_map/all_to_all | solution.py:504
  86.4 5.8 %select_rows.1.tile_ref = bf16[36,256,128]{2,1,0:T(8,128)(2,1)} custom-call(s32[16,256]{1,0:T(8,128)} %copy.18.tiles_ref, bf16[36,256,128]{2,1,0:T(8,128)(2,1)} %bitcast.12), custom_call_target="tpu_custom_call" | custom-call | tf_op jit(solution)/shard_map/select_rows/pallas_call | solution.py:264
  92.2 40.8 %conjugate.1 = (f32[6,256]{1,0:T(8,128)}, f32[6,256]{1,0:T(8,128)}) custom-call(bf16[36,256,128]{2,1,0:T(8,128)(2,1)} %select_rows.1.tile_ref, f32[6,8,256]{2,1,0:T(8,128)} %get-tuple-element.11.blocks_ref, f32[8,8,256]{2,1,0:T(8,128)} %get-tuple-element.12.right_ref), custom_call_target="tpu_custom_call" | custom-call | tf_op jit(solution)/shard_map/conjugate/pallas_call | solution.py:476
  133.0 1.3 copy.21
  134.3 1.3 copy.22
  (7 shorter events, 0.1 us)
Async XLA Ops:
  3.0 1.1 copy-start
  4.1 1.0 copy-start.1
  5.1 0.9 copy-start.3
  6.0 0.8 copy-start.4
  6.8 0.7 copy-start.5
  23.6 0.7 copy-start.2
  27.3 11.5 %copy-start.6 = (s32[2048]{0:T(1024)S(1)}, s32[2048]{0:T(1024)}, u32[]{:S(2)}) copy-start(s32[2048]{0:T(1024)} %param.11) | copy-start | bytes 24580
  27.3 55.2 %all-to-all-start = ((bf16[36,128,2,128]{3,2,0,1:T(2,128)(2,1)}), bf16[36,128,2,128]{3,2,0,1:T(2,128)(2,1)S(1)}, u32[]{:S(2)}, u32[]{:S(2)}) async-start(bf16[36,128,2,128]{3,2,0,1:T(2,128)(2,1)} %copy.16), calls=%async_computation | async-start | bytes 4718592 | tf_op jit(solution)/shard_map/all_to_all | solution.py:504

commit v2 on v0

v2 whole, which is shorter than its diff:
```python
import functools

import jax
import jax.numpy as jnp
from jax import lax
from jax.experimental import pallas as pl
from jax.experimental.pallas import tpu as pltpu
from jax.sharding import PartitionSpec as P

ITERS = 3
CAMERA_DAMPING = 1.0
POINT_DAMPING = 1.0

F32 = jnp.float32
BF16 = jnp.bfloat16
MESH = pl.DeviceIdType.MESH
LANES = 128

LINK = 36
PAIRS = [(x, y) for x in range(6) for y in range(x, 6)]
DIAG = len(PAIRS)
VALUES = 64
GRAD_AT = 24
SUM_ROWS = 32


def pair_index(x, y):
    return PAIRS.index((min(x, y), max(x, y)))


def dot3(first, second):
    total = first[0] * second[0]
    for k in range(1, len(first)):
        total = total + first[k] * second[k]
    return total


def point_chunk(cam_ref, pt_ref, res_ref, active, at):
    def cam(side, i):
        return [cam_ref[side, i, x, :, at].astype(F32) for x in range(6)]

    pa = [[pt_ref[0, i, k, :, at].astype(F32) for k in range(3)] for i in range(2)]
    pb = [[pt_ref[1, i, k, :, at].astype(F32) for k in range(3)] for i in range(2)]
    ea = [res_ref[0, i, :, at].astype(F32) for i in range(2)]
    eb = [res_ref[1, i, :, at].astype(F32) for i in range(2)]

    def hess(m, n):
        return pa[0][m] * pa[0][n] + pa[1][m] * pa[1][n] + (pb[0][m] * pb[0][n] + pb[1][m] * pb[1][n])

    v00, v11, v22 = (hess(k, k) + POINT_DAMPING for k in range(3))
    v01, v02, v12 = hess(0, 1), hess(0, 2), hess(1, 2)
    c00 = v11 * v22 - v12 * v12
    c01 = v02 * v12 - v01 * v22
    c02 = v01 * v12 - v02 * v11
    c11 = v00 * v22 - v02 * v02
    c12 = v01 * v02 - v00 * v12
    c22 = v00 * v11 - v01 * v01
    det = v00 * c00 + v01 * c01 + v02 * c02
    scale = 1.0 / det
    i00, i01, i02 = c00 * scale, c01 * scale, c02 * scale
    i11, i12, i22 = c11 * scale, c12 * scale, c22 * scale
    inv = [[i00, i01, i02], [i01, i11, i12], [i02, i12, i22]]
    q = [-(pa[0][k] * ea[0] + pa[1][k] * ea[1] + (pb[0][k] * eb[0] + pb[1][k] * eb[1])) for k in range(3)]
    pav = [[dot3(pa[i], inv[k]) for k in range(3)] for i in range(2)]
    pbv = [[dot3(pb[i], inv[k]) for k in range(3)] for i in range(2)]

    def schur(pv, p):
        n00 = (1.0 - dot3(pv[0], p[0])) * active
        n01 = -dot3(pv[0], p[1]) * active
        n11 = (1.0 - dot3(pv[1], p[1])) * active
        return [[n00, n01], [n01, n11]]

    naa, nbb = schur(pav, pa), schur(pbv, pb)
    mab = [[-dot3(pav[i], pb[j]) * active for j in range(2)] for i in range(2)]
    ga = [-(ea[i] + dot3(pav[i], q)) * active for i in range(2)]
    gb = [-(eb[i] + dot3(pbv[i], q)) * active for i in range(2)]
    ja = [cam(0, 0), cam(0, 1)]
    jb = [cam(1, 0), cam(1, 1)]

    def quad(left, middle, right, pairs):
        half = [[middle[i][0] * right[0][y] + middle[i][1] * right[1][y] for y in range(6)] for i in range(2)]
        return [left[0][x] * half[0][y] + left[1][x] * half[1][y] for x, y in pairs]

    link = quad(ja, mab, jb, [(x, y) for x in range(6) for y in range(6)])
    diag_other = quad(jb, nbb, jb, PAIRS)
    grad_other = [jb[0][x] * gb[0] + jb[1][x] * gb[1] for x in range(6)]
    diag_own = quad(ja, naa, ja, PAIRS)
    grad_own = [ja[0][x] * ga[0] + ja[1][x] * ga[1] for x in range(6)]
    return link + diag_other + grad_other, diag_own + grad_own


def slot_sum(buffer):
    total = buffer[0]
    for k in range(1, buffer.shape[0]):
        total = total + buffer[k]
    return total


def three_terms(value):
    first = value.astype(BF16)
    rest = value - first.astype(F32)
    second = rest.astype(BF16)
    third = (rest - second.astype(F32)).astype(BF16)
    return jnp.concatenate([first.astype(F32), second.astype(F32), third.astype(F32)], axis=0)


def row_masked(stacked, which):
    line = lax.broadcasted_iota(jnp.int32, stacked.shape, 0) & 7
    return jnp.where(line == which, stacked, 0.0).astype(BF16)


def start_along(axis, n, buffer, send, recv):
    me = lax.axis_index(axis)
    copies = []
    for k in range(1, n):
        copy = pltpu.make_async_remote_copy(
            src_ref=buffer.at[me],
            dst_ref=buffer.at[me],
            send_sem=send.at[k],
            recv_sem=recv.at[k],
            device_id={axis: lax.rem(me + k, n)},
            device_id_type=MESH,
        )
        copy.start()
        copies.append(copy)
    return copies


def finish(copies):
    for copy in copies:
        copy.wait()


def exclusive_or(first, second, bits):
    total = 0
    for k in range(bits):
        total = total + (1 << k) * lax.rem(first // (1 << k) + second // (1 << k), 2)
    return total


def whole_kernel(
    rows, cols,
    map_smem, count_smem, cam_hbm, pt_hbm, res_hbm, partner_hbm, map_ref,
    tile, update_ref, residual_ref,
    cam_ref, pt_ref, res_ref, partner_ref, rank,
    high, low, own_acc, lane_index, group_index, lhs, acc, weave,
    panel, received, sums, parts, selection,
    first_right, second_right, blocks,
    direction, remainder, answer, row_firsts, col_first, row_second, col_seconds,
    input_sems, panel_send, panel_recv, parts_send, parts_recv,
    first_send, first_recv, second_send, second_recv,
    send_row, recv_row, send_col, recv_col, send_row2, recv_row2, send_col2, recv_col2,
):
    row, col = lax.axis_index("row"), lax.axis_index("col")
    me = row * cols + col
    devices = rows * cols
    scn, points = partner_ref.shape
    chunks = points // LANES
    lines = map_ref.shape[0]
    groups = 8

    inputs = [
        pltpu.make_async_copy(source, target, input_sems.at[k])
        for k, (source, target) in enumerate(
            ((cam_hbm, cam_ref), (pt_hbm, pt_ref), (res_hbm, res_ref), (partner_hbm, partner_ref))
        )
    ]
    for copy in inputs:
        copy.start()

    barrier = pltpu.get_barrier_semaphore()

    def greet(k, carry):
        other = lax.rem(me + k, devices)
        pl.semaphore_signal(
            barrier, inc=1, device_id=(other // cols, lax.rem(other, cols)), device_id_type=MESH
        )
        return carry

    lax.fori_loop(1, devices, greet, 0)

    for s in range(scn):
        here = map_smem[me * scn + s]
        total = jnp.int32(0)
        for t in range(scn):
            if t != s:
                total = total + (map_smem[me * scn + t] < here).astype(jnp.int32)
        rank[s] = total

    def scalars_column(ref, offset, shape):
        line = lax.broadcasted_iota(jnp.int32, shape, 0)
        column = jnp.zeros(shape, jnp.int32)
        for s in range(shape[0]):
            column = jnp.where(line == s, ref[offset + s], column)
        return column

    counts = scalars_column(count_smem, 0, (scn, LANES))
    own_acc[...] = jnp.zeros_like(own_acc)
    acc[...] = jnp.zeros_like(acc)
    high[pl.ds((VALUES - 1) * scn, scn), :] = jnp.zeros((scn, points), F32)
    low[pl.ds((VALUES - 1) * scn, scn), :] = jnp.zeros((scn, points), F32)
    for copy in inputs:
        copy.wait()

    def chunk(j, carry):
        at = pl.ds(pl.multiple_of(j * LANES, LANES), LANES)
        slot = lax.broadcasted_iota(jnp.int32, (scn, LANES), 1) + j * LANES
        active = (slot < counts).astype(F32)
        values, own = point_chunk(cam_ref, pt_ref, res_ref, active, at)
        for v, value in enumerate(values):
            top = value.astype(BF16).astype(F32)
            high[pl.ds(v * scn, scn), at] = top
            low[pl.ds(v * scn, scn), at] = value - top
        for v, value in enumerate(own):
            own_acc[v] += value
        partner = partner_ref[:, at]
        which = partner & (LANES - 1)
        line = partner >> 7
        position = jnp.zeros((scn, LANES), jnp.int32)
        for h in range(lines):
            table_row = jnp.broadcast_to(map_ref[h : h + 1, :], (scn, LANES))
            position = jnp.where(line == h, jnp.take_along_axis(table_row, which, axis=1), position)
        column = position >> 7
        lane_index[:, at] = ((column >> 3) << 7) | (position & (LANES - 1))
        group_index[:, at] = column & 7
        return carry

    lax.fori_loop(0, chunks, chunk, 0)
    pl.semaphore_wait(barrier, devices - 1)

    def scatter(s, first, count):
        group_row = jnp.broadcast_to(group_index[pl.ds(s, 1), :], (groups, points))
        keep = group_row == lax.broadcasted_iota(jnp.int32, (groups, points), 0)
        lane_row = lane_index[pl.ds(s, 1), :]
        onehot = jnp.where(
            lane_row == lax.broadcasted_iota(jnp.int32, (256, points), 0), 1.0, 0.0
        ).astype(BF16)
        for part, source in enumerate((high, low)):
            for v in range(0, count, 2):
                pieces = [
                    jnp.where(
                        keep,
                        jnp.broadcast_to(source[pl.ds((first + v + k) * scn + s, 1), :], (groups, points)),
                        0.0,
                    )
                    for k in range(2)
                ]
                lhs[pl.ds((part * count + v) * groups, 2 * groups), :] = jnp.concatenate(pieces, axis=0).astype(BF16)
        result = lax.dot_general(
            lhs[: 2 * count * groups], onehot, (((1,), (1,)), ((), ())), preferred_element_type=F32
        )
        return result[: count * groups] + result[count * groups :]

    panel_view = panel.reshape(LINK, rows, 2, 2 * groups, LANES)

    def link_rows(k, carry):
        target = exclusive_or(row, k, 3)
        for slot in range(2):
            s = jnp.int32(0)
            for t in range(scn):
                s = jnp.where(rank[t] == target * 2 + slot, t, s)
            result = scatter(s, 0, LINK)
            for x in range(LINK):
                for b in range(2):
                    weave[pl.ds((x * 2 + b) * 2 * groups + slot, groups, stride=2), :] = result[
                        x * groups : (x + 1) * groups, b * LANES : (b + 1) * LANES
                    ]
        panel_view[:, target] = weave[...].reshape(LINK, 2, 2 * groups, LANES).astype(BF16)
        return carry

    def send_rows(k, carry):
        target = exclusive_or(row, k, 3)

        def send(j, inner):
            column = exclusive_or(col, j, 4)
            there = target * cols + column

            @pl.when(k * cols + j > 0)
            def _():
                pltpu.make_async_remote_copy(
                    src_ref=panel.at[:, there],
                    dst_ref=received.at[:, me],
                    send_sem=panel_send,
                    recv_sem=panel_recv,
                    device_id=(target, column),
                    device_id_type=MESH,
                ).start()

            return inner

        return lax.fori_loop(0, cols, send, carry)

    def link_and_send(k, carry):
        link_rows(k, 0)
        send_rows(k, 0)
        return carry

    lax.fori_loop(0, 2, link_and_send, 0)
    received[:, me] = panel[:, me]

    def other_sums(s, carry):
        result = scatter(s, LINK, VALUES - LINK)
        for b in range(2):
            acc[pl.ds(b * (VALUES - LINK) * groups, (VALUES - LINK) * groups), :] += result[
                :, b * LANES : (b + 1) * LANES
            ]
        return carry

    lax.fori_loop(0, scn, other_sums, 0)
    lanes = lax.broadcasted_iota(jnp.int32, (scn, LANES), 1)
    own_table = jnp.zeros((scn, LANES), F32)
    for v in range(DIAG + 6):
        total = jnp.sum(own_acc[v], axis=1, keepdims=True)
        own_table = jnp.where(lanes == (v if v < DIAG else GRAD_AT + v - DIAG), total, own_table)
    own_table = own_table.T[:SUM_ROWS]
    own_at = scalars_column(map_smem, me * scn, (scn, LANES))
    zeros = jnp.zeros((3, LANES), F32)
    for b in range(2):
        for h in range(groups):
            column = b * groups + h
            spread = (own_at == lanes + column * LANES).astype(F32)
            own_sum = lax.dot_general(
                own_table, spread, (((1,), (0,)), ((), ())),
                precision=lax.Precision.HIGHEST, preferred_element_type=F32,
            )
            other = acc[pl.ds(b * (VALUES - LINK) * groups + h, VALUES - LINK, stride=groups), :]
            sums[column // 2, :, (column % 2) * LANES : (column % 2 + 1) * LANES] = own_sum + jnp.concatenate(
                [other[:DIAG], zeros, other[DIAG : DIAG + 6], zeros[:2]], axis=0
            )
    part_copies = []
    for k in range(1, rows):
        there = lax.rem(row + k, rows)
        copy = pltpu.make_async_remote_copy(
            src_ref=sums.at[there],
            dst_ref=parts.at[row],
            send_sem=parts_send.at[k],
            recv_sem=parts_recv.at[k],
            device_id={"row": there},
            device_id_type=MESH,
        )
        copy.start()
        part_copies.append(copy)
    parts[row] = sums[row]

    lax.fori_loop(2, 4, link_and_send, 0)
    lax.fori_loop(4, rows, link_rows, 0)

    finish(part_copies)
    total = slot_sum(parts)
    first_right[col] = total[GRAD_AT : GRAD_AT + 8]
    copies = start_along("col", cols, first_right, first_send, first_recv)
    lax.fori_loop(4, 6, send_rows, 0)
    line = lax.broadcasted_iota(jnp.int32, (8, 256), 0)
    for y in range(6):
        block = jnp.zeros((8, 256), F32)
        for x in range(6):
            v = pair_index(x, y)
            block = jnp.where(line == x, jnp.broadcast_to(total[v : v + 1], (8, 256)), block)
        blocks[y] = block

    offset = map_ref[...] - row * 256
    inside = (offset >= 0) & (offset < 256)
    lane = lax.broadcasted_iota(jnp.int32, (lines, LANES), 1)
    least = jnp.where(inside, offset, 256)
    for span in (1, 2, 4, 8):
        ahead = pltpu.roll(least, LANES - span, axis=1)
        behind = pltpu.roll(least, span, axis=1)
        least = jnp.minimum(least, jnp.where((lane & span) == 0, ahead, behind))
    later = (offset != least).astype(jnp.int32)
    source = (lax.broadcasted_iota(jnp.int32, (lines, LANES), 0) * 8 + (lane >> 4)) * 2 + later
    place = jnp.where(inside, offset, -1)
    source = jnp.where(inside, source, -1)
    deep = lax.broadcasted_iota(jnp.int32, (256, LANES), 0)
    chosen = jnp.zeros((256, 256), F32)
    for h in range(lines):
        place_hot = jnp.where(place[h : h + 1] == deep, 1.0, 0.0).astype(BF16)
        source_hot = jnp.where(source[h : h + 1] == deep, 1.0, 0.0).astype(BF16)
        chosen = chosen + lax.dot_general(
            place_hot, source_hot, (((1,), (1,)), ((), ())), preferred_element_type=F32
        )
    selection[...] = chosen.astype(BF16)

    finish(copies)
    second_right[row] = slot_sum(first_right)
    copies = start_along("row", rows, second_right, second_send, second_recv)
    lax.fori_loop(6, rows, send_rows, 0)
    finish(copies)
    start = second_right[...]
    direction[...] = start
    remainder[...] = start
    answer[...] = jnp.zeros_like(answer)

    def inner_product(first, second):
        total = first[0] * second[0]
        for r in range(1, rows):
            total = total + first[r] * second[r]
        return jnp.sum(jnp.sum(total, axis=0, keepdims=True), axis=1, keepdims=True)

    norm_start = inner_product(start, start)

    landed = received.at[:, pl.ds(0, devices - 1)]
    pltpu.make_async_copy(landed, landed, panel_recv).wait()
    received_view = received.reshape(LINK, 2 * devices, LANES)

    def select(x, carry):
        pair = jnp.concatenate([received_view[2 * x], received_view[2 * x + 1]], axis=1)
        chosen_rows = jnp.dot(selection[...], pair, preferred_element_type=F32).astype(BF16)
        tile[2 * x] = chosen_rows[:, :LANES]
        tile[2 * x + 1] = chosen_rows[:, LANES:]
        return carry

    lax.fori_loop(0, LINK // 2, select, 0)

    def iteration(step, norm_now):
        parity = lax.rem(step, 2)
        row_first, col_second = row_firsts.at[parity], col_seconds.at[parity]
        rows_part = direction[row]
        cols_part = direction[col // 2, :, pl.ds(pl.multiple_of(lax.rem(col, 2) * LANES, LANES), LANES)]
        row_terms, col_terms = three_terms(rows_part), three_terms(cols_part)
        col_lhs = [row_masked(col_terms, y) for y in range(6)]
        row_lhs = [row_masked(row_terms, x) for x in range(6)]
        line_rows = lax.broadcasted_iota(jnp.int32, (8, 256), 0)
        line_cols = lax.broadcasted_iota(jnp.int32, (8, LANES), 0)
        forward = jnp.zeros((8, 256), F32)
        for y in range(6):
            forward = forward + blocks[y] * jnp.broadcast_to(rows_part[y : y + 1], (8, 256))
        for x in range(6):
            total = None
            for y in range(6):
                part = lax.dot_general(
                    col_lhs[y], tile[x * 6 + y], (((1,), (1,)), ((), ())), preferred_element_type=F32
                )
                total = part if total is None else total + part
            forward = forward + jnp.where(line_rows == x, jnp.sum(total, axis=0, keepdims=True), 0.0)
        row_first[col] = forward
        copies = start_along("col", cols, row_first, send_row.at[parity], recv_row.at[parity])
        backward = jnp.zeros((8, LANES), F32)
        for y in range(6):
            total = None
            for x in range(6):
                part = jnp.dot(row_lhs[x], tile[x * 6 + y], preferred_element_type=F32)
                total = part if total is None else total + part
            backward = backward + jnp.where(line_cols == y, jnp.sum(total, axis=0, keepdims=True), 0.0)
        col_first[row] = backward
        finish(start_along("row", rows, col_first, send_col, recv_col))
        col_second[col] = slot_sum(col_first)
        second_copies = start_along("col", cols, col_second, send_col2.at[parity], recv_col2.at[parity])
        finish(copies)
        row_second[row] = slot_sum(row_first)
        finish(start_along("row", rows, row_second, send_row2, recv_row2))
        finish(second_copies)
        held = direction[...]
        image = CAMERA_DAMPING * held + row_second[...]
        back = jnp.stack(
            [jnp.concatenate([col_second[2 * r], col_second[2 * r + 1]], axis=1) for r in range(rows)], axis=0
        )
        image = image + back
        step_size = norm_now / inner_product(held, image)
        answer[...] = answer[...] + step_size[None] * held
        left = remainder[...] - step_size[None] * image
        remainder[...] = left
        norm_next = inner_product(left, left)
        direction[...] = left + (norm_next / norm_now)[None] * held
        return norm_next

    lax.fori_loop(0, ITERS, iteration, norm_start)
    update_ref[...] = answer[row][:6]
    residual_ref[...] = remainder[row][:6]
    sent = panel.at[:, pl.ds(0, devices - 1)]
    pltpu.make_async_copy(sent, sent, panel_send).wait()


def store_kernel(*refs):
    count = len(refs) // 2
    sems = refs[-1]
    copies = [pltpu.make_async_copy(refs[k], refs[count + k], sems.at[k]) for k in range(count)]
    for copy in copies:
        copy.start()
    for copy in copies:
        copy.wait()


def store(arrays):
    return pl.pallas_call(
        store_kernel,
        in_specs=[pl.BlockSpec(memory_space=pltpu.VMEM)] * len(arrays),
        out_specs=[pl.BlockSpec(memory_space=pltpu.HBM)] * len(arrays),
        out_shape=[jax.ShapeDtypeStruct(array.shape, array.dtype) for array in arrays],
        scratch_shapes=[pltpu.SemaphoreType.DMA((len(arrays),))],
        compiler_params=pltpu.CompilerParams(vmem_limit_bytes=8 * 1024 * 1024),
        name="store",
    )(*arrays)


def shards(cam_jac, pt_jac, resid, partner, count, tile_map):
    rows, cols = lax.axis_size("row"), lax.axis_size("col")
    scn, points = partner.shape
    devices = rows * cols
    groups = 8
    dma = pltpu.SemaphoreType.DMA
    vmem = pltpu.VMEM
    smem_spec = pl.BlockSpec(memory_space=pltpu.SMEM)
    vmem_spec = pl.BlockSpec(memory_space=pltpu.VMEM)
    hbm_spec = pl.BlockSpec(memory_space=pltpu.HBM)
    coupling, update, residual = pl.pallas_call(
        functools.partial(whole_kernel, rows, cols),
        in_specs=[smem_spec, smem_spec, hbm_spec, hbm_spec, hbm_spec, hbm_spec, vmem_spec],
        out_specs=[vmem_spec] * 3,
        out_shape=[
            jax.ShapeDtypeStruct((LINK, 256, LANES), BF16),
            jax.ShapeDtypeStruct((6, 256), F32),
            jax.ShapeDtypeStruct((6, 256), F32),
        ],
        scratch_shapes=[
            vmem(cam_jac.shape, BF16),
            vmem(pt_jac.shape, BF16),
            vmem(resid.shape, BF16),
            vmem(partner.shape, jnp.int32),
            pltpu.SMEM((scn,), jnp.int32),
            vmem((VALUES * scn, points), F32),
            vmem((VALUES * scn, points), F32),
            vmem((DIAG + 6, scn, LANES), F32),
            vmem((scn, points), jnp.int32),
            vmem((scn, points), jnp.int32),
            vmem((2 * LINK * groups, points), BF16),
            vmem((2 * (VALUES - LINK) * groups, LANES), F32),
            vmem((LINK * 2 * 2 * groups, LANES), F32),
            vmem((LINK, devices, 2, LANES), BF16),
            vmem((LINK, devices, 2, LANES), BF16),
            vmem((rows, SUM_ROWS, 256), F32),
            vmem((rows, SUM_ROWS, 256), F32),
            vmem((256, 256), BF16),
            vmem((cols, 8, 256), F32),
            vmem((rows, 8, 256), F32),
            vmem((6, 8, 256), F32),
            vmem((rows, 8, 256), F32),
            vmem((rows, 8, 256), F32),
            vmem((rows, 8, 256), F32),
            vmem((2, cols, 8, 256), F32),
            vmem((rows, 8, LANES), F32),
            vmem((rows, 8, 256), F32),
            vmem((2, cols, 8, LANES), F32),
            dma((4,)), dma, dma, dma((rows,)), dma((rows,)),
            dma((cols,)), dma((cols,)), dma((rows,)), dma((rows,)),
            dma((2, cols)), dma((2, cols)), dma((rows,)), dma((rows,)),
            dma((rows,)), dma((rows,)), dma((2, cols)), dma((2, cols)),
        ],
        compiler_params=pltpu.CompilerParams(
            collective_id=0, has_side_effects=True, vmem_limit_bytes=48 * 1024 * 1024
        ),
        name="bundle",
    )(
        *(
            pltpu.with_memory_space_constraint(array, pltpu.HBM)
            for array in (tile_map, count, cam_jac, pt_jac, resid, partner, tile_map.reshape(-1, LANES))
        )
    )
    coupling, update, residual = store([coupling, update, residual])
    return coupling.reshape(6, 6, 256, LANES), update, residual


def solution(mesh):
    return jax.shard_map(
        shards,
        mesh=mesh,
        in_specs=(
            P(None, None, None, ("row", "col"), None),
            P(None, None, None, ("row", "col"), None),
            P(None, None, ("row", "col"), None),
            P(("row", "col"), None),
            P(("row", "col")),
            P(),
        ),
        out_specs=(P(None, None, "row", "col"), P(None, "row"), P(None, "row")),
        check_vma=False,
    )
```

time: 591 us -> 110 us (0.19); the launches traced: 580 us -> 109 us
  blocking collectives: 268 us -> 0 us
  Pallas kernels: 0 us -> 109 us
  matrix products: 87.4 us -> 0 us
  waiting for transfers between devices: 77.3 us -> 0 us
  local copies, waits for them, and re-layouts: 59.7 us -> 0 us
  other arithmetic: 54.1 us -> 0 us
  between operations: 21.6 us -> 0.64 us
  starting transfers between devices: 11.5 us -> 0 us
    psum x4 -> x0, blocking collectives: 268 us -> none  [the longest x3 191 us: tile_products(): return lax.psum(spread, ('row', 'col'))]
    pallas_call x0 -> x2, Pallas kernels: none -> 109 us  [the longest x1 107 us: shards(): pl.pallas_call(functools.partial(whole_kernel, rows, cols), in_specs=[sme...]
    dot_general x25 -> x0, matrix products: 87.4 us -> none  [the longest x16 66.2 us: scene_sums(): jnp.dot(scene_values, onehot, precision=lax.Precision.HIGHEST, preferred_...]
    psum x1 -> x0, waiting for transfers between devices: 77.3 us -> none  [shards(): diag_all, grad_all = lax.psum((diag_part, grad_part), ('row', 'col'))]
    dynamic_slice x39 -> x0, local copies, waits for them, and re-layouts: 44.6 us -> none  [the longest x32 44.5 us: shards(): per_scene = lax.map(scene_sums, (values, partner))]
    reduce_sum x35 -> x0, other arithmetic: 42.1 us -> none  [the longest x16 20.3 us: scene_sums(): tile_other = jnp.sum(jnp.where(hits, tile_map[None, :], 0), axis=1)]
    all_to_all x1 -> x0, starting transfers between devices: 11.5 us -> none  [shards(): lax.all_to_all(shaped, ('row', 'col'), split_axis=1, concat_axis=1, tiled...]
  transfers between devices with their start and end apart: 2 -> 0, of which waited for: 1 -> 0; matrix products, arithmetic and copies ran while one was open for 2% -> 0% of each run, Pallas kernels for 0% -> 0%
where the time goes in v2:
time: 110 us; the launch traced here: 109 us
  Pallas kernels  109 us (99%)
    pallas_call x1, Pallas kernels, shards(): pl.pallas_call(functools.partial(whole_kernel, rows, cols), in_specs=[sme...  107 us

profile of v2, /device:TPU:1, one launch (start us, length us, event | category | flops | bytes accessed | tf_op | source)
XLA Modules:
  0.0 109.4 jit_solution(16222350948035017268)
XLA Ops:
  0.6 107.3 %bundle.1 = (bf16[36,256,128]{2,1,0:T(8,128)(2,1)S(1)}, f32[6,256]{1,0:T(8,128)S(1)}, f32[6,256]{1,0:T(8,128)S(1)}) custom-call(s32[2048]{0:T(1024)} %map_smem.1, s32[16]{0:T(128)} %count_smem.1, bf16[2,2,6,16,1024]{4,3,2,1,0:T(8,128)(2,1)} %cam_hbm.1, bf16[2,2,3,16,1024]{4,3,2,1,0:T(8,128)(2,1)} %pt_hbm.1, bf16[2,2,16,1024]{3,2,1,0:T(8,128)(2,1)} %res_hbm.1, ...), custom_call_target="tpu_custom_call" | custom-call | tf_op jit(solution)/shard_map/bundle/pallas_call | solution.py:505
  108.0 1.4 %store.1 = (bf16[36,256,128]{2,1,0:T(8,128)(2,1)}, f32[6,256]{1,0:T(8,128)}, f32[6,256]{1,0:T(8,128)}) custom-call(bf16[36,256,128]{2,1,0:T(8,128)(2,1)S(1)} %get-tuple-element.9.refs_0_, f32[6,256]{1,0:T(8,128)S(1)} %get-tuple-element.10.refs_1_, f32[6,256]{1,0:T(8,128)S(1)} %get-tuple-element.11.refs_2_), custom_call_target="tpu_custom_call" | custom-call | tf_op jit(solution)/shard_map/store/pallas_call | solution.py:484

commit v3 on v2

--- a/solution.py
+++ b/solution.py
@@ -228,7 +228,7 @@
     lax.fori_loop(0, chunks, chunk, 0)
     pl.semaphore_wait(barrier, devices - 1)
 
-    def scatter(s, first, count):
+    def scatter(s, first, count, buffer):
         group_row = jnp.broadcast_to(group_index[pl.ds(s, 1), :], (groups, points))
         keep = group_row == lax.broadcasted_iota(jnp.int32, (groups, points), 0)
         lane_row = lane_index[pl.ds(s, 1), :]
@@ -245,21 +245,23 @@
                     )
                     for k in range(2)
                 ]
-                lhs[pl.ds((part * count + v) * groups, 2 * groups), :] = jnp.concatenate(pieces, axis=0).astype(BF16)
+                lhs[buffer, pl.ds((part * count + v) * groups, 2 * groups), :] = jnp.concatenate(pieces, axis=0).astype(BF16)
         result = lax.dot_general(
-            lhs[: 2 * count * groups], onehot, (((1,), (1,)), ((), ())), preferred_element_type=F32
+            lhs[buffer, : 2 * count * groups], onehot, (((1,), (1,)), ((), ())), preferred_element_type=F32
         )
         return result[: count * groups] + result[count * groups :]
 
+    first_target = exclusive_or(row, lax.rem(col, rows), 3)
+
     panel_view = panel.reshape(LINK, rows, 2, 2 * groups, LANES)
 
     def link_rows(k, carry):
-        target = exclusive_or(row, k, 3)
+        target = exclusive_or(first_target, k, 3)
         for slot in range(2):
             s = jnp.int32(0)
             for t in range(scn):
                 s = jnp.where(rank[t] == target * 2 + slot, t, s)
-            result = scatter(s, 0, LINK)
+            result = scatter(s, 0, LINK, slot)
             for x in range(LINK):
                 for b in range(2):
                     weave[pl.ds((x * 2 + b) * 2 * groups + slot, groups, stride=2), :] = result[
@@ -268,15 +270,18 @@
         panel_view[:, target] = weave[...].reshape(LINK, 2, 2 * groups, LANES).astype(BF16)
         return carry
 
+    col_flips = [(1 << k) * (1 - 2 * lax.rem(col // (1 << k), 2)) for k in range(4)]
+
     def send_rows(k, carry):
-        target = exclusive_or(row, k, 3)
-
-        def send(j, inner):
-            column = exclusive_or(col, j, 4)
+        target = exclusive_or(first_target, k, 3)
+        for j in range(cols):
+            column = col
+            for bit in range(4):
+                if j >> bit & 1:
+                    column = column + col_flips[bit]
             there = target * cols + column
 
-            @pl.when(k * cols + j > 0)
-            def _():
+            def send():
                 pltpu.make_async_remote_copy(
                     src_ref=panel.at[:, there],
                     dst_ref=received.at[:, me],
@@ -286,27 +291,28 @@
                     device_id_type=MESH,
                 ).start()
 
-            return inner
-
-        return lax.fori_loop(0, cols, send, carry)
+            if j == 0:
+                pl.when(target != row)(send)
+            else:
+                send()
+        return carry
 
     def link_and_send(k, carry):
         link_rows(k, 0)
         send_rows(k, 0)
         return carry
 
-    lax.fori_loop(0, 2, link_and_send, 0)
-    received[:, me] = panel[:, me]
-
-    def other_sums(s, carry):
-        result = scatter(s, LINK, VALUES - LINK)
+    lax.fori_loop(0, rows, link_and_send, 0)
+
+    def other_sums(pair, carry):
+        result = sum(scatter(pair * 2 + k, LINK, VALUES - LINK, k) for k in range(2))
         for b in range(2):
             acc[pl.ds(b * (VALUES - LINK) * groups, (VALUES - LINK) * groups), :] += result[
                 :, b * LANES : (b + 1) * LANES
             ]
         return carry
 
-    lax.fori_loop(0, scn, other_sums, 0)
+    lax.fori_loop(0, scn // 2, other_sums, 0)
     lanes = lax.broadcasted_iota(jnp.int32, (scn, LANES), 1)
     own_table = jnp.zeros((scn, LANES), F32)
     for v in range(DIAG + 6):
@@ -342,21 +348,7 @@
         part_copies.append(copy)
     parts[row] = sums[row]
 
-    lax.fori_loop(2, 4, link_and_send, 0)
-    lax.fori_loop(4, rows, link_rows, 0)
-
-    finish(part_copies)
-    total = slot_sum(parts)
-    first_right[col] = total[GRAD_AT : GRAD_AT + 8]
-    copies = start_along("col", cols, first_right, first_send, first_recv)
-    lax.fori_loop(4, 6, send_rows, 0)
-    line = lax.broadcasted_iota(jnp.int32, (8, 256), 0)
-    for y in range(6):
-        block = jnp.zeros((8, 256), F32)
-        for x in range(6):
-            v = pair_index(x, y)
-            block = jnp.where(line == x, jnp.broadcast_to(total[v : v + 1], (8, 256)), block)
-        blocks[y] = block
+    received[:, me] = panel[:, me]
 
     offset = map_ref[...] - row * 256
     inside = (offset >= 0) & (offset < 256)
@@ -380,11 +372,37 @@
         )
     selection[...] = chosen.astype(BF16)
 
+    finish(part_copies)
+    total = slot_sum(parts)
+    first_right[col] = total[GRAD_AT : GRAD_AT + 8]
+    copies = start_along("col", cols, first_right, first_send, first_recv)
+    line = lax.broadcasted_iota(jnp.int32, (8, 256), 0)
+    for y in range(6):
+        block = jnp.zeros((8, 256), F32)
+        for x in range(6):
+            v = pair_index(x, y)
+            block = jnp.where(line == x, jnp.broadcast_to(total[v : v + 1], (8, 256)), block)
+        blocks[y] = block
+
+
+    landed = received.at[:, pl.ds(0, devices - 1)]
+    pltpu.make_async_copy(landed, landed, panel_recv).wait()
+    received_view = received.reshape(LINK, 2 * devices, LANES)
+
+    def select(block, carry):
+        for k in range(6):
+            x = (block * 6 + k) * 2
+            pair = jnp.concatenate([received_view[x], received_view[x + 1]], axis=1)
+            chosen_rows = jnp.dot(selection[...], pair, preferred_element_type=F32).astype(BF16)
+            tile[x] = chosen_rows[:, :LANES]
+            tile[x + 1] = chosen_rows[:, LANES:]
+        return carry
+
+    lax.fori_loop(0, LINK // 12, select, 0)
+
     finish(copies)
     second_right[row] = slot_sum(first_right)
-    copies = start_along("row", rows, second_right, second_send, second_recv)
-    lax.fori_loop(6, rows, send_rows, 0)
-    finish(copies)
+    finish(start_along("row", rows, second_right, second_send, second_recv))
     start = second_right[...]
     direction[...] = start
     remainder[...] = start
@@ -397,19 +415,6 @@
         return jnp.sum(jnp.sum(total, axis=0, keepdims=True), axis=1, keepdims=True)
 
     norm_start = inner_product(start, start)
-
-    landed = received.at[:, pl.ds(0, devices - 1)]
-    pltpu.make_async_copy(landed, landed, panel_recv).wait()
-    received_view = received.reshape(LINK, 2 * devices, LANES)
-
-    def select(x, carry):
-        pair = jnp.concatenate([received_view[2 * x], received_view[2 * x + 1]], axis=1)
-        chosen_rows = jnp.dot(selection[...], pair, preferred_element_type=F32).astype(BF16)
-        tile[2 * x] = chosen_rows[:, :LANES]
-        tile[2 * x + 1] = chosen_rows[:, LANES:]
-        return carry
-
-    lax.fori_loop(0, LINK // 2, select, 0)
 
     def iteration(step, norm_now):
         parity = lax.rem(step, 2)
@@ -522,7 +527,7 @@
             vmem((DIAG + 6, scn, LANES), F32),
             vmem((scn, points), jnp.int32),
             vmem((scn, points), jnp.int32),
-            vmem((2 * LINK * groups, points), BF16),
+            vmem((2, 2 * LINK * groups, points), BF16),
             vmem((2 * (VALUES - LINK) * groups, LANES), F32),
             vmem((LINK * 2 * 2 * groups, LANES), F32),
             vmem((LINK, devices, 2, LANES), BF16),

time: 110 us -> 97.1 us (0.88)
  Pallas kernels: 109 us -> 96.2 us
    pallas_call x1, Pallas kernels: 107 us -> 94.8 us  [shards(): pl.pallas_call(functools.partial(whole_kernel, rows, cols), in_specs=[sme...]
where the time goes in v3:
time: 97.1 us; the launch traced here: 96.9 us
  Pallas kernels  96.2 us (99%)
    pallas_call x1, Pallas kernels, shards(): pl.pallas_call(functools.partial(whole_kernel, rows, cols), in_specs=[sme...  94.8 us

profile of v3, /device:TPU:1, one launch (start us, length us, event | category | flops | bytes accessed | tf_op | source)
XLA Modules:
  0.0 96.9 jit_solution(4713289522718165937)
XLA Ops:
  0.6 94.8 %bundle.1 = (bf16[36,256,128]{2,1,0:T(8,128)(2,1)S(1)}, f32[6,256]{1,0:T(8,128)S(1)}, f32[6,256]{1,0:T(8,128)S(1)}) custom-call(s32[2048]{0:T(1024)} %map_smem.1, s32[16]{0:T(128)} %count_smem.1, bf16[2,2,6,16,1024]{4,3,2,1,0:T(8,128)(2,1)} %cam_hbm.1, bf16[2,2,3,16,1024]{4,3,2,1,0:T(8,128)(2,1)} %pt_hbm.1, bf16[2,2,16,1024]{3,2,1,0:T(8,128)(2,1)} %res_hbm.1, ...), custom_call_target="tpu_custom_call" | custom-call | tf_op jit(solution)/shard_map/bundle/pallas_call | solution.py:510
  95.4 1.4 %store.1 = (bf16[36,256,128]{2,1,0:T(8,128)(2,1)}, f32[6,256]{1,0:T(8,128)}, f32[6,256]{1,0:T(8,128)}) custom-call(bf16[36,256,128]{2,1,0:T(8,128)(2,1)S(1)} %get-tuple-element.9.refs_0_, f32[6,256]{1,0:T(8,128)S(1)} %get-tuple-element.10.refs_1_, f32[6,256]{1,0:T(8,128)S(1)} %get-tuple-element.11.refs_2_), custom_call_target="tpu_custom_call" | custom-call | tf_op jit(solution)/shard_map/store/pallas_call | solution.py:489

commit v4 on v3

--- a/solution.py
+++ b/solution.py
@@ -109,26 +109,36 @@
     return jnp.where(line == which, stacked, 0.0).astype(BF16)
 
 
-def start_along(axis, n, buffer, send, recv):
-    me = lax.axis_index(axis)
-    copies = []
-    for k in range(1, n):
-        copy = pltpu.make_async_remote_copy(
+def xor_flips(index, bits):
+    return [(1 << k) * (1 - 2 * lax.rem(index // (1 << k), 2)) for k in range(bits)]
+
+
+def flipped(index, flips, which):
+    for k, flip in enumerate(flips):
+        if which >> k & 1:
+            index = index + flip
+    return index
+
+
+COL_ORDER = (11, 10, 9, 8, 7, 6, 15, 14, 3, 2, 5, 4, 13, 12, 1)
+ROW_ORDER = (5, 4, 3, 7, 1, 2, 6)
+
+
+def start_along(axis, me, flips, order, buffer, send, recv):
+    for which in order:
+        pltpu.make_async_remote_copy(
             src_ref=buffer.at[me],
             dst_ref=buffer.at[me],
-            send_sem=send.at[k],
-            recv_sem=recv.at[k],
-            device_id={axis: lax.rem(me + k, n)},
+            send_sem=send,
+            recv_sem=recv,
+            device_id={axis: flipped(me, flips, which)},
             device_id_type=MESH,
-        )
-        copy.start()
-        copies.append(copy)
-    return copies
-
-
-def finish(copies):
-    for copy in copies:
-        copy.wait()
+        ).start()
+
+
+def wait_slots(buffer, sem):
+    slots = buffer.at[pl.ds(0, buffer.shape[0] - 1)]
+    pltpu.make_async_copy(slots, slots, sem).wait()
 
 
 def exclusive_or(first, second, bits):
@@ -140,11 +150,11 @@
 
 def whole_kernel(
     rows, cols,
-    map_smem, count_smem, cam_hbm, pt_hbm, res_hbm, partner_hbm, map_ref,
+    map_hbm, count_hbm, cam_hbm, pt_hbm, res_hbm, partner_hbm, table_hbm,
     tile, update_ref, residual_ref,
-    cam_ref, pt_ref, res_ref, partner_ref, rank,
+    map_smem, count_smem, map_ref, cam_ref, pt_ref, res_ref, partner_ref, rank,
     high, low, own_acc, lane_index, group_index, lhs, acc, weave,
-    panel, received, sums, parts, selection,
+    panel, received, sums, grads, grad_parts, parts, selection,
     first_right, second_right, blocks,
     direction, remainder, answer, row_firsts, col_first, row_second, col_seconds,
     input_sems, panel_send, panel_recv, parts_send, parts_recv,
@@ -154,6 +164,9 @@
     row, col = lax.axis_index("row"), lax.axis_index("col")
     me = row * cols + col
     devices = rows * cols
+    row_flips, col_flips = xor_flips(row, 3), xor_flips(col, 4)
+    spread_row = functools.partial(start_along, "col", col, col_flips, COL_ORDER)
+    spread_col = functools.partial(start_along, "row", row, row_flips, ROW_ORDER)
     scn, points = partner_ref.shape
     chunks = points // LANES
     lines = map_ref.shape[0]
@@ -162,7 +175,10 @@
     inputs = [
         pltpu.make_async_copy(source, target, input_sems.at[k])
         for k, (source, target) in enumerate(
-            ((cam_hbm, cam_ref), (pt_hbm, pt_ref), (res_hbm, res_ref), (partner_hbm, partner_ref))
+            (
+                (map_hbm, map_smem), (count_hbm, count_smem), (table_hbm, map_ref),
+                (pt_hbm, pt_ref), (cam_hbm, cam_ref), (res_hbm, res_ref), (partner_hbm, partner_ref),
+            )
         )
     ]
     for copy in inputs:
@@ -178,6 +194,12 @@
         return carry
 
     lax.fori_loop(1, devices, greet, 0)
+    own_acc[...] = jnp.zeros_like(own_acc)
+    acc[...] = jnp.zeros_like(acc)
+    high[pl.ds((VALUES - 1) * scn, scn), :] = jnp.zeros((scn, points), F32)
+    low[pl.ds((VALUES - 1) * scn, scn), :] = jnp.zeros((scn, points), F32)
+    for copy in inputs:
+        copy.wait()
 
     for s in range(scn):
         here = map_smem[me * scn + s]
@@ -195,12 +217,6 @@
         return column
 
     counts = scalars_column(count_smem, 0, (scn, LANES))
-    own_acc[...] = jnp.zeros_like(own_acc)
-    acc[...] = jnp.zeros_like(acc)
-    high[pl.ds((VALUES - 1) * scn, scn), :] = jnp.zeros((scn, points), F32)
-    low[pl.ds((VALUES - 1) * scn, scn), :] = jnp.zeros((scn, points), F32)
-    for copy in inputs:
-        copy.wait()
 
     def chunk(j, carry):
         at = pl.ds(pl.multiple_of(j * LANES, LANES), LANES)
@@ -226,7 +242,6 @@
         return carry
 
     lax.fori_loop(0, chunks, chunk, 0)
-    pl.semaphore_wait(barrier, devices - 1)
 
     def scatter(s, first, count, buffer):
         group_row = jnp.broadcast_to(group_index[pl.ds(s, 1), :], (groups, points))
@@ -270,15 +285,10 @@
         panel_view[:, target] = weave[...].reshape(LINK, 2, 2 * groups, LANES).astype(BF16)
         return carry
 
-    col_flips = [(1 << k) * (1 - 2 * lax.rem(col // (1 << k), 2)) for k in range(4)]
-
     def send_rows(k, carry):
         target = exclusive_or(first_target, k, 3)
         for j in range(cols):
-            column = col
-            for bit in range(4):
-                if j >> bit & 1:
-                    column = column + col_flips[bit]
+            column = flipped(col, col_flips, j)
             there = target * cols + column
 
             def send():
@@ -302,17 +312,10 @@
         send_rows(k, 0)
         return carry
 
-    lax.fori_loop(0, rows, link_and_send, 0)
-
-    def other_sums(pair, carry):
-        result = sum(scatter(pair * 2 + k, LINK, VALUES - LINK, k) for k in range(2))
-        for b in range(2):
-            acc[pl.ds(b * (VALUES - LINK) * groups, (VALUES - LINK) * groups), :] += result[
-                :, b * LANES : (b + 1) * LANES
-            ]
-        return carry
-
-    lax.fori_loop(0, scn // 2, other_sums, 0)
+    link_rows(0, 0)
+    pl.semaphore_wait(barrier, devices - 1)
+    send_rows(0, 0)
+
     lanes = lax.broadcasted_iota(jnp.int32, (scn, LANES), 1)
     own_table = jnp.zeros((scn, LANES), F32)
     for v in range(DIAG + 6):
@@ -320,35 +323,67 @@
         own_table = jnp.where(lanes == (v if v < DIAG else GRAD_AT + v - DIAG), total, own_table)
     own_table = own_table.T[:SUM_ROWS]
     own_at = scalars_column(map_smem, me * scn, (scn, LANES))
+    for column in range(2 * groups):
+        spread = (own_at == lanes + column * LANES).astype(F32)
+        sums[column // 2, :, (column % 2) * LANES : (column % 2 + 1) * LANES] = lax.dot_general(
+            own_table, spread, (((1,), (0,)), ((), ())),
+            precision=lax.Precision.HIGHEST, preferred_element_type=F32,
+        )
+
+    def other_sums(first, count):
+        acc[...] = jnp.zeros_like(acc)
+
+        def pair_sums(pair, carry):
+            result = sum(scatter(pair * 2 + k, first, count, k) for k in range(2))
+            for b in range(2):
+                acc[pl.ds(b * (VALUES - LINK) * groups, count * groups), :] += result[
+                    :, b * LANES : (b + 1) * LANES
+                ]
+            return carry
+
+        lax.fori_loop(0, scn // 2, pair_sums, 0)
+
+    def other_rows(column, count):
+        return acc[pl.ds(column // groups * (VALUES - LINK) * groups + column % groups, count, stride=groups), :]
+
+    other_sums(LINK + DIAG, 6)
     zeros = jnp.zeros((3, LANES), F32)
-    for b in range(2):
-        for h in range(groups):
-            column = b * groups + h
-            spread = (own_at == lanes + column * LANES).astype(F32)
-            own_sum = lax.dot_general(
-                own_table, spread, (((1,), (0,)), ((), ())),
-                precision=lax.Precision.HIGHEST, preferred_element_type=F32,
-            )
-            other = acc[pl.ds(b * (VALUES - LINK) * groups + h, VALUES - LINK, stride=groups), :]
-            sums[column // 2, :, (column % 2) * LANES : (column % 2 + 1) * LANES] = own_sum + jnp.concatenate(
-                [other[:DIAG], zeros, other[DIAG : DIAG + 6], zeros[:2]], axis=0
-            )
-    part_copies = []
-    for k in range(1, rows):
-        there = lax.rem(row + k, rows)
-        copy = pltpu.make_async_remote_copy(
-            src_ref=sums.at[there],
-            dst_ref=parts.at[row],
-            send_sem=parts_send.at[k],
-            recv_sem=parts_recv.at[k],
-            device_id={"row": there},
-            device_id_type=MESH,
-        )
-        copy.start()
-        part_copies.append(copy)
-    parts[row] = sums[row]
-
+    for column in range(2 * groups):
+        lane = slice((column % 2) * LANES, (column % 2 + 1) * LANES)
+        grads[column // 2, :, lane] = sums[column // 2, GRAD_AT:, lane] + jnp.concatenate(
+            [other_rows(column, 6), zeros[:2]], axis=0
+        )
+
+    def start_parts(source, target, send, recv):
+        for which in ROW_ORDER:
+            there = flipped(row, row_flips, which)
+            pltpu.make_async_remote_copy(
+                src_ref=source.at[there],
+                dst_ref=target.at[row],
+                send_sem=send,
+                recv_sem=recv,
+                device_id={"row": there},
+                device_id_type=MESH,
+            ).start()
+
+    start_parts(grads, grad_parts, parts_send.at[0], parts_recv.at[0])
+    grad_parts[row] = grads[row]
+    lax.fori_loop(1, 3, link_and_send, 0)
+    wait_slots(grad_parts, parts_recv.at[0])
+    first_right[col] = slot_sum(grad_parts)
+    spread_row(first_right, first_send, first_recv)
+    lax.fori_loop(3, rows, link_and_send, 0)
     received[:, me] = panel[:, me]
+    wait_slots(first_right, first_recv)
+    second_right[row] = slot_sum(first_right)
+    spread_col(second_right, second_send, second_recv)
+
+    other_sums(LINK, DIAG + 1)
+    for column in range(2 * groups):
+        lane = slice((column % 2) * LANES, (column % 2 + 1) * LANES)
+        sums[column // 2, :GRAD_AT, lane] += jnp.concatenate([other_rows(column, DIAG), zeros], axis=0)
+    start_parts(sums.at[:, pl.ds(0, GRAD_AT)], parts, parts_send.at[1], parts_recv.at[1])
+    parts[row] = sums[row, :GRAD_AT]
 
     offset = map_ref[...] - row * 256
     inside = (offset >= 0) & (offset < 256)
@@ -372,10 +407,21 @@
         )
     selection[...] = chosen.astype(BF16)
 
-    finish(part_copies)
+    wait_slots(second_right, second_recv)
+    start = second_right[...]
+    direction[...] = start
+    remainder[...] = start
+    answer[...] = jnp.zeros_like(answer)
+
+    def inner_product(first, second):
+        total = first[0] * second[0]
+        for r in range(1, rows):
+            total = total + first[r] * second[r]
+        return jnp.sum(jnp.sum(total, axis=0, keepdims=True), axis=1, keepdims=True)
+
+    norm_start = inner_product(start, start)
+    wait_slots(parts, parts_recv.at[1])
     total = slot_sum(parts)
-    first_right[col] = total[GRAD_AT : GRAD_AT + 8]
-    copies = start_along("col", cols, first_right, first_send, first_recv)
     line = lax.broadcasted_iota(jnp.int32, (8, 256), 0)
     for y in range(6):
         block = jnp.zeros((8, 256), F32)
@@ -399,22 +445,6 @@
         return carry
 
     lax.fori_loop(0, LINK // 12, select, 0)
-
-    finish(copies)
-    second_right[row] = slot_sum(first_right)
-    finish(start_along("row", rows, second_right, second_send, second_recv))
-    start = second_right[...]
-    direction[...] = start
-    remainder[...] = start
-    answer[...] = jnp.zeros_like(answer)
-
-    def inner_product(first, second):
-        total = first[0] * second[0]
-        for r in range(1, rows):
-            total = total + first[r] * second[r]
-        return jnp.sum(jnp.sum(total, axis=0, keepdims=True), axis=1, keepdims=True)
-
-    norm_start = inner_product(start, start)
 
     def iteration(step, norm_now):
         parity = lax.rem(step, 2)
@@ -438,7 +468,7 @@
                 total = part if total is None else total + part
             forward = forward + jnp.where(line_rows == x, jnp.sum(total, axis=0, keepdims=True), 0.0)
         row_first[col] = forward
-        copies = start_along("col", cols, row_first, send_row.at[parity], recv_row.at[parity])
+        spread_row(row_first, send_row.at[parity], recv_row.at[parity])
         backward = jnp.zeros((8, LANES), F32)
         for y in range(6):
             total = None
@@ -447,13 +477,19 @@
                 total = part if total is None else total + part
             backward = backward + jnp.where(line_cols == y, jnp.sum(total, axis=0, keepdims=True), 0.0)
         col_first[row] = backward
-        finish(start_along("row", rows, col_first, send_col, recv_col))
+        spread_col(col_first, send_col, recv_col)
+        wait_slots(col_first, recv_col)
         col_second[col] = slot_sum(col_first)
-        second_copies = start_along("col", cols, col_second, send_col2.at[parity], recv_col2.at[parity])
-        finish(copies)
+        spread_row(col_second, send_col2.at[parity], recv_col2.at[parity])
+        wait_slots(row_first, recv_row.at[parity])
         row_second[row] = slot_sum(row_first)
-        finish(start_along("row", rows, row_second, send_row2, recv_row2))
-        finish(second_copies)
+        spread_col(row_second, send_row2, recv_row2)
+        wait_slots(row_second, recv_row2)
+        wait_slots(col_second, recv_col2.at[parity])
+        wait_slots(row_first, send_row.at[parity])
+        wait_slots(col_first, send_col)
+        wait_slots(row_second, send_row2)
+        wait_slots(col_second, send_col2.at[parity])
         held = direction[...]
         image = CAMERA_DAMPING * held + row_second[...]
         back = jnp.stack(
@@ -473,6 +509,10 @@
     residual_ref[...] = remainder[row][:6]
     sent = panel.at[:, pl.ds(0, devices - 1)]
     pltpu.make_async_copy(sent, sent, panel_send).wait()
+    wait_slots(grad_parts, parts_send.at[0])
+    wait_slots(parts, parts_send.at[1])
+    wait_slots(first_right, first_send)
+    wait_slots(second_right, second_send)
 
 
 def store_kernel(*refs):
@@ -504,12 +544,11 @@
     groups = 8
     dma = pltpu.SemaphoreType.DMA
     vmem = pltpu.VMEM
-    smem_spec = pl.BlockSpec(memory_space=pltpu.SMEM)
     vmem_spec = pl.BlockSpec(memory_space=pltpu.VMEM)
     hbm_spec = pl.BlockSpec(memory_space=pltpu.HBM)
     coupling, update, residual = pl.pallas_call(
         functools.partial(whole_kernel, rows, cols),
-        in_specs=[smem_spec, smem_spec, hbm_spec, hbm_spec, hbm_spec, hbm_spec, vmem_spec],
+        in_specs=[hbm_spec] * 7,
         out_specs=[vmem_spec] * 3,
         out_shape=[
             jax.ShapeDtypeStruct((LINK, 256, LANES), BF16),
@@ -517,6 +556,9 @@
             jax.ShapeDtypeStruct((6, 256), F32),
         ],
         scratch_shapes=[
+            pltpu.SMEM(tile_map.shape, jnp.int32),
+            pltpu.SMEM(count.shape, jnp.int32),
+            vmem((tile_map.shape[0] // LANES, LANES), jnp.int32),
             vmem(cam_jac.shape, BF16),
             vmem(pt_jac.shape, BF16),
             vmem(resid.shape, BF16),
@@ -533,7 +575,9 @@
             vmem((LINK, devices, 2, LANES), BF16),
             vmem((LINK, devices, 2, LANES), BF16),
             vmem((rows, SUM_ROWS, 256), F32),
-            vmem((rows, SUM_ROWS, 256), F32),
+            vmem((rows, 8, 256), F32),
+            vmem((rows, 8, 256), F32),
+            vmem((rows, GRAD_AT, 256), F32),
             vmem((256, 256), BF16),
             vmem((cols, 8, 256), F32),
             vmem((rows, 8, 256), F32),
@@ -545,10 +589,9 @@
             vmem((rows, 8, LANES), F32),
             vmem((rows, 8, 256), F32),
             vmem((2, cols, 8, LANES), F32),
-            dma((4,)), dma, dma, dma((rows,)), dma((rows,)),
-            dma((cols,)), dma((cols,)), dma((rows,)), dma((rows,)),
-            dma((2, cols)), dma((2, cols)), dma((rows,)), dma((rows,)),
-            dma((rows,)), dma((rows,)), dma((2, cols)), dma((2, cols)),
+            dma((7,)), dma, dma, dma((2,)), dma((2,)),
+            dma, dma, dma, dma,
+            dma((2,)), dma((2,)), dma, dma, dma, dma, dma((2,)), dma((2,)),
         ],
         compiler_params=pltpu.CompilerParams(
             collective_id=0, has_side_effects=True, vmem_limit_bytes=48 * 1024 * 1024

time: 97.1 us -> 91 us (0.937)
  Pallas kernels: 96.2 us -> 90.2 us
    pallas_call x1, Pallas kernels: 94.8 us -> 88.8 us  [shards(): pl.pallas_call(functools.partial(whole_kernel, rows, cols), in_specs=[hbm...]
where the time goes in v4:
time: 91 us; the launch traced here: 90.9 us
  Pallas kernels  90.2 us (99%)
    pallas_call x1, Pallas kernels, shards(): pl.pallas_call(functools.partial(whole_kernel, rows, cols), in_specs=[hbm...  88.8 us

profile of v4, /device:TPU:1, one launch (start us, length us, event | category | flops | bytes accessed | tf_op | source)
XLA Modules:
  0.0 90.9 jit_solution(9019394323301165076)
XLA Ops:
  0.6 88.8 %bundle.1 = (bf16[36,256,128]{2,1,0:T(8,128)(2,1)S(1)}, f32[6,256]{1,0:T(8,128)S(1)}, f32[6,256]{1,0:T(8,128)S(1)}) custom-call(s32[2048]{0:T(1024)} %map_hbm.1, s32[16]{0:T(128)} %count_hbm.1, bf16[2,2,6,16,1024]{4,3,2,1,0:T(8,128)(2,1)} %cam_hbm.1, bf16[2,2,3,16,1024]{4,3,2,1,0:T(8,128)(2,1)} %pt_hbm.1, bf16[2,2,16,1024]{3,2,1,0:T(8,128)(2,1)} %res_hbm.1, ...), custom_call_target="tpu_custom_call" | custom-call | tf_op jit(solution)/shard_map/bundle/pallas_call | solution.py:549
  89.4 1.4 %store.1 = (bf16[36,256,128]{2,1,0:T(8,128)(2,1)}, f32[6,256]{1,0:T(8,128)}, f32[6,256]{1,0:T(8,128)}) custom-call(bf16[36,256,128]{2,1,0:T(8,128)(2,1)S(1)} %get-tuple-element.9.refs_0_, f32[6,256]{1,0:T(8,128)S(1)} %get-tuple-element.10.refs_1_, f32[6,256]{1,0:T(8,128)S(1)} %get-tuple-element.11.refs_2_), custom_call_target="tpu_custom_call" | custom-call | tf_op jit(solution)/shard_map/store/pallas_call | solution.py:529

commit v5 on v4

--- a/solution.py
+++ b/solution.py
@@ -287,7 +287,7 @@
 
     def send_rows(k, carry):
         target = exclusive_or(first_target, k, 3)
-        for j in range(cols):
+        for j in COL_ORDER + (0,):
             column = flipped(col, col_flips, j)
             there = target * cols + column
 
@@ -368,11 +368,11 @@
 
     start_parts(grads, grad_parts, parts_send.at[0], parts_recv.at[0])
     grad_parts[row] = grads[row]
-    lax.fori_loop(1, 3, link_and_send, 0)
+    lax.fori_loop(1, 4, link_and_send, 0)
     wait_slots(grad_parts, parts_recv.at[0])
     first_right[col] = slot_sum(grad_parts)
     spread_row(first_right, first_send, first_recv)
-    lax.fori_loop(3, rows, link_and_send, 0)
+    lax.fori_loop(4, rows, link_and_send, 0)
     received[:, me] = panel[:, me]
     wait_slots(first_right, first_recv)
     second_right[row] = slot_sum(first_right)
@@ -407,6 +407,21 @@
         )
     selection[...] = chosen.astype(BF16)
 
+    landed = received.at[:, pl.ds(0, devices - 1)]
+    pltpu.make_async_copy(landed, landed, panel_recv).wait()
+    received_view = received.reshape(LINK, 2 * devices, LANES)
+
+    def select(block, carry):
+        for k in range(6):
+            x = (block * 6 + k) * 2
+            pair = jnp.concatenate([received_view[x], received_view[x + 1]], axis=1)
+            chosen_rows = jnp.dot(selection[...], pair, preferred_element_type=F32).astype(BF16)
+            tile[x] = chosen_rows[:, :LANES]
+            tile[x + 1] = chosen_rows[:, LANES:]
+        return carry
+
+    lax.fori_loop(0, LINK // 12, select, 0)
+
     wait_slots(second_right, second_recv)
     start = second_right[...]
     direction[...] = start
@@ -429,22 +444,6 @@
             v = pair_index(x, y)
             block = jnp.where(line == x, jnp.broadcast_to(total[v : v + 1], (8, 256)), block)
         blocks[y] = block
-
-
-    landed = received.at[:, pl.ds(0, devices - 1)]
-    pltpu.make_async_copy(landed, landed, panel_recv).wait()
-    received_view = received.reshape(LINK, 2 * devices, LANES)
-
-    def select(block, carry):
-        for k in range(6):
-            x = (block * 6 + k) * 2
-            pair = jnp.concatenate([received_view[x], received_view[x + 1]], axis=1)
-            chosen_rows = jnp.dot(selection[...], pair, preferred_element_type=F32).astype(BF16)
-            tile[x] = chosen_rows[:, :LANES]
-            tile[x + 1] = chosen_rows[:, LANES:]
-        return carry
-
-    lax.fori_loop(0, LINK // 12, select, 0)
 
     def iteration(step, norm_now):
         parity = lax.rem(step, 2)

time: 91 us -> 89.9 us (0.988)
  Pallas kernels: 90.2 us -> 89.1 us
    pallas_call x1, Pallas kernels: 88.8 us -> 87.7 us  [shards(): pl.pallas_call(functools.partial(whole_kernel, rows, cols), in_specs=[hbm...]
where the time goes in v5:
time: 89.9 us; the launch traced here: 89.8 us
  Pallas kernels  89.1 us (99%)
    pallas_call x1, Pallas kernels, shards(): pl.pallas_call(functools.partial(whole_kernel, rows, cols), in_specs=[hbm...  87.7 us

profile of v5, /device:TPU:1, one launch (start us, length us, event | category | flops | bytes accessed | tf_op | source)
XLA Modules:
  0.0 89.8 jit_solution(525336187216372726)
XLA Ops:
  0.6 87.7 %bundle.1 = (bf16[36,256,128]{2,1,0:T(8,128)(2,1)S(1)}, f32[6,256]{1,0:T(8,128)S(1)}, f32[6,256]{1,0:T(8,128)S(1)}) custom-call(s32[2048]{0:T(1024)} %map_hbm.1, s32[16]{0:T(128)} %count_hbm.1, bf16[2,2,6,16,1024]{4,3,2,1,0:T(8,128)(2,1)} %cam_hbm.1, bf16[2,2,3,16,1024]{4,3,2,1,0:T(8,128)(2,1)} %pt_hbm.1, bf16[2,2,16,1024]{3,2,1,0:T(8,128)(2,1)} %res_hbm.1, ...), custom_call_target="tpu_custom_call" | custom-call | tf_op jit(solution)/shard_map/bundle/pallas_call | solution.py:548
  88.3 1.4 %store.1 = (bf16[36,256,128]{2,1,0:T(8,128)(2,1)}, f32[6,256]{1,0:T(8,128)}, f32[6,256]{1,0:T(8,128)}) custom-call(bf16[36,256,128]{2,1,0:T(8,128)(2,1)S(1)} %get-tuple-element.9.refs_0_, f32[6,256]{1,0:T(8,128)S(1)} %get-tuple-element.10.refs_1_, f32[6,256]{1,0:T(8,128)S(1)} %get-tuple-element.11.refs_2_), custom_call_target="tpu_custom_call" | custom-call | tf_op jit(solution)/shard_map/store/pallas_call | solution.py:528

commit v6 on v5

--- a/solution.py
+++ b/solution.py
@@ -187,13 +187,19 @@
     barrier = pltpu.get_barrier_semaphore()
 
     def greet(k, carry):
-        other = lax.rem(me + k, devices)
-        pl.semaphore_signal(
-            barrier, inc=1, device_id=(other // cols, lax.rem(other, cols)), device_id_type=MESH
-        )
+        target = exclusive_or(row, k, 3)
+        for j in COL_ORDER + (0,):
+
+            def signal(column=flipped(col, col_flips, j)):
+                pl.semaphore_signal(barrier, inc=1, device_id=(target, column), device_id_type=MESH)
+
+            if j == 0:
+                pl.when(k > 0)(signal)
+            else:
+                signal()
         return carry
 
-    lax.fori_loop(1, devices, greet, 0)
+    lax.fori_loop(0, rows, greet, 0)
     own_acc[...] = jnp.zeros_like(own_acc)
     acc[...] = jnp.zeros_like(acc)
     high[pl.ds((VALUES - 1) * scn, scn), :] = jnp.zeros((scn, points), F32)
@@ -459,12 +465,10 @@
         for y in range(6):
             forward = forward + blocks[y] * jnp.broadcast_to(rows_part[y : y + 1], (8, 256))
         for x in range(6):
-            total = None
-            for y in range(6):
-                part = lax.dot_general(
-                    col_lhs[y], tile[x * 6 + y], (((1,), (1,)), ((), ())), preferred_element_type=F32
-                )
-                total = part if total is None else total + part
+            wide = jnp.concatenate([tile[x * 6 + y] for y in range(6)], axis=1)
+            total = lax.dot_general(
+                jnp.concatenate(col_lhs, axis=1), wide, (((1,), (1,)), ((), ())), preferred_element_type=F32
+            )
             forward = forward + jnp.where(line_rows == x, jnp.sum(total, axis=0, keepdims=True), 0.0)
         row_first[col] = forward
         spread_row(row_first, send_row.at[parity], recv_row.at[parity])

time: 89.9 us -> 88 us (0.979)
  Pallas kernels: 89.1 us -> 87.3 us
    pallas_call x1, Pallas kernels: 87.7 us -> 85.8 us  [shards(): pl.pallas_call(functools.partial(whole_kernel, rows, cols), in_specs=[hbm...]
where the time goes in v6:
time: 88 us; the launch traced here: 87.9 us
  Pallas kernels  87.3 us (99%)
    pallas_call x1, Pallas kernels, shards(): pl.pallas_call(functools.partial(whole_kernel, rows, cols), in_specs=[hbm...  85.8 us

profile of v6, /device:TPU:1, one launch (start us, length us, event | category | flops | bytes accessed | tf_op | source)
XLA Modules:
  0.0 87.9 jit_solution(8694888143584123711)
XLA Ops:
  0.6 85.8 %bundle.1 = (bf16[36,256,128]{2,1,0:T(8,128)(2,1)S(1)}, f32[6,256]{1,0:T(8,128)S(1)}, f32[6,256]{1,0:T(8,128)S(1)}) custom-call(s32[2048]{0:T(1024)} %map_hbm.1, s32[16]{0:T(128)} %count_hbm.1, bf16[2,2,6,16,1024]{4,3,2,1,0:T(8,128)(2,1)} %cam_hbm.1, bf16[2,2,3,16,1024]{4,3,2,1,0:T(8,128)(2,1)} %pt_hbm.1, bf16[2,2,16,1024]{3,2,1,0:T(8,128)(2,1)} %res_hbm.1, ...), custom_call_target="tpu_custom_call" | custom-call | tf_op jit(solution)/shard_map/bundle/pallas_call | solution.py:552
  86.5 1.4 %store.1 = (bf16[36,256,128]{2,1,0:T(8,128)(2,1)}, f32[6,256]{1,0:T(8,128)}, f32[6,256]{1,0:T(8,128)}) custom-call(bf16[36,256,128]{2,1,0:T(8,128)(2,1)S(1)} %get-tuple-element.9.refs_0_, f32[6,256]{1,0:T(8,128)S(1)} %get-tuple-element.10.refs_1_, f32[6,256]{1,0:T(8,128)S(1)} %get-tuple-element.11.refs_2_), custom_call_target="tpu_custom_call" | custom-call | tf_op jit(solution)/shard_map/store/pallas_call | solution.py:532

commit v7 on v6

--- a/solution.py
+++ b/solution.py
@@ -250,8 +250,9 @@
     lax.fori_loop(0, chunks, chunk, 0)
 
     def scatter(s, first, count, buffer):
-        group_row = jnp.broadcast_to(group_index[pl.ds(s, 1), :], (groups, points))
-        keep = group_row == lax.broadcasted_iota(jnp.int32, (groups, points), 0)
+        group_row = jnp.broadcast_to(group_index[pl.ds(s, 1), :].astype(F32).astype(BF16), (2 * groups, points))
+        group_line = lax.broadcasted_iota(jnp.int32, (2 * groups, points), 0) & (groups - 1)
+        keep = group_row == group_line.astype(F32).astype(BF16)
         lane_row = lane_index[pl.ds(s, 1), :]
         onehot = jnp.where(
             lane_row == lax.broadcasted_iota(jnp.int32, (256, points), 0), 1.0, 0.0
@@ -259,14 +260,12 @@
         for part, source in enumerate((high, low)):
             for v in range(0, count, 2):
                 pieces = [
-                    jnp.where(
-                        keep,
-                        jnp.broadcast_to(source[pl.ds((first + v + k) * scn + s, 1), :], (groups, points)),
-                        0.0,
-                    )
+                    jnp.broadcast_to(source[pl.ds((first + v + k) * scn + s, 1), :], (groups, points))
                     for k in range(2)
                 ]
-                lhs[buffer, pl.ds((part * count + v) * groups, 2 * groups), :] = jnp.concatenate(pieces, axis=0).astype(BF16)
+                lhs[buffer, pl.ds((part * count + v) * groups, 2 * groups), :] = jnp.where(
+                    keep, jnp.concatenate(pieces, axis=0).astype(BF16), jnp.zeros((), BF16)
+                )
         result = lax.dot_general(
             lhs[buffer, : 2 * count * groups], onehot, (((1,), (1,)), ((), ())), preferred_element_type=F32
         )

time: 88 us -> 88 us (level)
  no operation moved by 1% of the time
where the time goes in v7:
time: 88 us; the launch traced here: 87.9 us
  Pallas kernels  87.2 us (99%)
    pallas_call x1, Pallas kernels, shards(): pl.pallas_call(functools.partial(whole_kernel, rows, cols), in_specs=[hbm...  85.8 us

profile of v7, /device:TPU:1, one launch (start us, length us, event | category | flops | bytes accessed | tf_op | source)
XLA Modules:
  0.0 87.9 jit_solution(4729803549184738962)
XLA Ops:
  0.6 85.8 %bundle.1 = (bf16[36,256,128]{2,1,0:T(8,128)(2,1)S(1)}, f32[6,256]{1,0:T(8,128)S(1)}, f32[6,256]{1,0:T(8,128)S(1)}) custom-call(s32[2048]{0:T(1024)} %map_hbm.1, s32[16]{0:T(128)} %count_hbm.1, bf16[2,2,6,16,1024]{4,3,2,1,0:T(8,128)(2,1)} %cam_hbm.1, bf16[2,2,3,16,1024]{4,3,2,1,0:T(8,128)(2,1)} %pt_hbm.1, bf16[2,2,16,1024]{3,2,1,0:T(8,128)(2,1)} %res_hbm.1, ...), custom_call_target="tpu_custom_call" | custom-call | tf_op jit(solution)/shard_map/bundle/pallas_call | solution.py:551
  86.4 1.4 %store.1 = (bf16[36,256,128]{2,1,0:T(8,128)(2,1)}, f32[6,256]{1,0:T(8,128)}, f32[6,256]{1,0:T(8,128)}) custom-call(bf16[36,256,128]{2,1,0:T(8,128)(2,1)S(1)} %get-tuple-element.9.refs_0_, f32[6,256]{1,0:T(8,128)S(1)} %get-tuple-element.10.refs_1_, f32[6,256]{1,0:T(8,128)S(1)} %get-tuple-element.11.refs_2_), custom_call_target="tpu_custom_call" | custom-call | tf_op jit(solution)/shard_map/store/pallas_call | solution.py:531
